TPU v7x, 32 devices: a whole 2x2x4 slice. The times are simulated.
32 devices in a mesh: gx: 8 (over y, x, core), gy: 4 (over z).
Axes of the slice: x: 2, y: 2, z: 4, core: 2. Of those that a mesh axis runs over, the one named last changes fastest.
Arguments:
- basis: float32 [32, 128, 64, 256], P(None, 'gx', 'gy'), may hold values from -0.09375 to 0.09375
- reaction: float32 [128, 64, 256], P('gx', 'gy'), may hold values from 0.5 to 4
Outputs:
- extended: float32 [32, 128, 64, 256], P(None, 'gx', 'gy')
- coarse: float32 [32, 5, 32, 32], replicated
All inputs are finite; a program needn't handle non-finite values.
Results may differ from a plain program's by a relative error of at most 0.000071.
Values sent between devices are 32-bit elements; how exact they have to be, the bound alone decides.
A program may use at most 128 MiB of HBM per device.

v0:
```python
import functools

import jax
import jax.numpy as jnp
from jax import lax
from jax.experimental import pallas as pl
from jax.experimental.pallas import tpu as pltpu
from jax.sharding import PartitionSpec as P

SWEEPS = 4
OMEGA = 0.8
GROUP = 8
LANES = 128


def passed_along(block, axis, distance):
    devices = range(lax.axis_size(axis))
    route = [(i - distance, i) for i in devices if i - distance in devices]
    return lax.ppermute(block, axis, route)


def along_z(field, lane):
    zero = jnp.zeros_like(field[0])
    back = [pltpu.roll(piece, 1, 1) for piece in field]
    ahead = [pltpu.roll(piece, LANES - 1, 1) for piece in field]
    sums = []
    for h in range(len(field)):
        below = jnp.where(lane == 0, back[h - 1] if h else zero, back[h])
        above = jnp.where(lane == LANES - 1, ahead[h + 1] if h + 1 < len(field) else zero, ahead[h])
        sums.append(below + above)
    return sums


def pieces(ref, x, y):
    parts = ref.shape[-1] // LANES
    return [ref[x, y, :, h * LANES:(h + 1) * LANES] for h in range(parts)]


def halves(value):
    high = value.astype(jnp.bfloat16).astype(jnp.float32)
    return jnp.concatenate([value, value - high], axis=0).astype(jnp.bfloat16)


def extend_kernel(basis, reaction, extended, product, upper, first, second, weight, centre, left, right):
    _, cx, cy, cz = basis.shape
    parts = cz // LANES
    group = pl.program_id(0)
    lane = lax.broadcasted_iota(jnp.int32, (GROUP, LANES), 1)

    @pl.when(group == 0)
    def _():
        blank = jnp.zeros((cy, GROUP, cz), jnp.float32)
        for buffer in (first,):
            buffer[0] = blank
            buffer[cx + 1] = blank

        @pl.loop(0, cx)
        def _(x):
            whole = 6.0 + reaction[x]
            scaled = OMEGA / whole
            for y in range(cy):
                centre[x, y] = jnp.broadcast_to(whole[y:y + 1], (GROUP, cz))
                weight[x, y] = jnp.broadcast_to(scaled[y:y + 1], (GROUP, cz))

    @pl.loop(0, cx, unroll=2)
    def _(x):
        for y in range(0, cy, GROUP):
            turned = jnp.swapaxes(basis[:, x, y:y + GROUP, :], 0, 1)
            first[x + 1, y:y + GROUP] = turned
            if y == 0:
                second[x + 1, 0] = turned[0]
            if y == cy - GROUP:
                second[x + 1, cy - 1] = turned[GROUP - 1]

    second[1] = first[1]
    second[cx] = first[cx]

    buffers = (first, second)
    for sweep in range(SWEEPS):
        source, target = buffers[sweep % 2], buffers[(sweep + 1) % 2]

        @pl.loop(2, cx, unroll=7)
        def _(x):
            before, here = pieces(source, x, 0), pieces(source, x, 1)
            for y in range(1, cy - 1):
                after = pieces(source, x, y + 1)
                down, up = pieces(source, x - 1, y), pieces(source, x + 1, y)
                scale = pieces(weight, x - 1, y)
                beside = along_z(here, lane)
                for h in range(parts):
                    total = (down[h] + up[h]) + (before[h] + after[h]) + beside[h]
                    target[x, y, :, h * LANES:(h + 1) * LANES] = (
                        (1.0 - OMEGA) * here[h] + scale[h] * total
                    )
                before, here = here, after

    final = buffers[SWEEPS % 2]
    rows = pl.ds(pl.multiple_of(group * 2 * GROUP, 2 * GROUP), 2 * GROUP)

    @pl.loop(1, cx + 1, unroll=2)
    def _(x):
        before, here = None, pieces(final, x, 0)
        for y in range(cy):
            after = pieces(final, x, y + 1) if y + 1 < cy else None
            down, up = pieces(final, x - 1, y), pieces(final, x + 1, y)
            whole = pieces(centre, x - 1, y)
            beside = along_z(here, lane)
            for h in range(parts):
                total = (down[h] + up[h]) + beside[h]
                if before is not None:
                    total = total + before[h]
                if after is not None:
                    total = total + after[h]
                applied = whole[h] * here[h] - total
                left[x - 1, y * parts + h, rows, :] = halves(here[h])
                right[x - 1, y * parts + h, rows, :] = halves(applied)
            before, here = here, after
        for y in range(0, cy, GROUP):
            extended[:, x - 1, y:y + GROUP, :] = jnp.swapaxes(final[x, y:y + GROUP], 0, 1)

    for x in range(0, cx, GROUP):
        upper[:, x:x + GROUP, :] = jnp.swapaxes(final[x + 1:x + 1 + GROUP, cy - 1], 0, 1)

    @pl.when(group == pl.num_programs(0) - 1)
    def _():
        def add(x, total):
            one = jnp.concatenate([left[x, i] for i in range(cy * parts)], axis=1)
            other = jnp.concatenate([right[x, i] for i in range(cy * parts)], axis=1)
            return total + lax.dot_general(
                one, other, (((1,), (1,)), ((), ())), preferred_element_type=jnp.float32
            )

        size = product.shape[0]
        product[...] = lax.fori_loop(0, cx, add, jnp.zeros((size, size), jnp.float32))


def extend(basis, reaction):
    width, cx, cy, cz = basis.shape
    field = (cx + 2, cy, GROUP, cz)
    factors = pltpu.VMEM((cx, cy * cz // LANES, 2 * width, LANES), jnp.bfloat16)
    block = pl.BlockSpec((GROUP, cx, cy, cz), lambda g: (g, 0, 0, 0))
    return pl.pallas_call(
        extend_kernel,
        grid=(width // GROUP,),
        in_specs=[block, pl.BlockSpec((cx, cy, cz), lambda g: (0, 0, 0))],
        out_specs=[
            block,
            pl.BlockSpec((2 * width, 2 * width), lambda g: (0, 0)),
            pl.BlockSpec((GROUP, cx, cz), lambda g: (g, 0, 0)),
        ],
        out_shape=[
            jax.ShapeDtypeStruct(basis.shape, jnp.float32),
            jax.ShapeDtypeStruct((2 * width, 2 * width), jnp.float32),
            jax.ShapeDtypeStruct((width, cx, cz), jnp.float32),
        ],
        scratch_shapes=[
            pltpu.VMEM(field, jnp.float32),
            pltpu.VMEM(field, jnp.float32),
            pltpu.VMEM((cx, cy, GROUP, cz), jnp.float32),
            pltpu.VMEM((cx, cy, GROUP, cz), jnp.float32),
            factors,
            factors,
        ],
        compiler_params=pltpu.CompilerParams(vmem_limit_bytes=56 * 2**20),
        cost_estimate=pl.CostEstimate(
            flops=60 * basis.size, bytes_accessed=8 * basis.size, transcendentals=0
        ),
    )(basis, reaction)


def face_kernel(basis, face):
    face[...] = basis[:, :, 0, :]


def lower_face(basis):
    width, cx, _, cz = basis.shape
    return pl.pallas_call(
        face_kernel,
        grid=(width // GROUP,),
        in_specs=[pl.BlockSpec((GROUP, cx, GROUP, cz), lambda g: (g, 0, 0, 0))],
        out_specs=pl.BlockSpec((GROUP, cx, cz), lambda g: (g, 0, 0)),
        out_shape=jax.ShapeDtypeStruct((width, cx, cz), jnp.float32),
    )(basis)


def couple(own, other):
    width = own.shape[0]
    return -jnp.dot(
        own.reshape(width, -1),
        other.reshape(width, -1).T,
        precision=lax.Precision.HIGHEST,
        preferred_element_type=jnp.float32,
    )


def packed(block):
    rows = block.shape[0] * block.shape[1] // LANES
    return jnp.concatenate(
        [block[i:i + rows] for i in range(0, block.shape[0], rows)], axis=1
    )


def unpacked(tile, width):
    return jnp.concatenate(
        [tile[:, i:i + width] for i in range(0, LANES, width)], axis=0
    )


def spread_kernel(ngx, ngy, product, plus_x, plus_y, coarse, held, send_y, recv_y, send_x, recv_x):
    gx, gy = lax.axis_index("gx"), lax.axis_index("gy")
    width = plus_x.shape[0]

    barrier = pltpu.get_barrier_semaphore()
    for d in range(1, ngy):
        pl.semaphore_signal(
            barrier, inc=1, device_id=(gx, lax.rem(gy + d, ngy)), device_id_type=pl.DeviceIdType.MESH
        )
    for d in range(1, ngx):
        pl.semaphore_signal(
            barrier, inc=1, device_id=(lax.rem(gx + d, ngx), gy), device_id_type=pl.DeviceIdType.MESH
        )

    span = 2 * GROUP
    rows = jnp.concatenate(
        [product[i:i + GROUP] + product[i + GROUP:i + span] for i in range(0, 2 * width, span)], axis=0
    )
    diag = jnp.concatenate(
        [rows[:, i:i + GROUP] + rows[:, i + GROUP:i + span] for i in range(0, 2 * width, span)], axis=1
    )
    held[gx, gy, 0] = packed(diag)
    held[gx, gy, 1] = packed(plus_x[...])
    held[gx, gy, 2] = packed(plus_y[...])
    for y in range(ngy):
        coarse[y, 1] = jnp.zeros((width, width), jnp.float32)
    coarse[0, 3] = jnp.zeros((width, width), jnp.float32)
    pl.semaphore_wait(barrier, ngx + ngy - 2)

    def over_y(owner, peer):
        piece = held.at[gx, owner]
        return pltpu.make_async_remote_copy(
            src_ref=piece, dst_ref=piece, send_sem=send_y.at[peer], recv_sem=recv_y.at[owner],
            device_id=(gx, peer), device_id_type=pl.DeviceIdType.MESH,
        )

    def over_x(row, owner, peer):
        piece = held.at[row, owner]
        return pltpu.make_async_remote_copy(
            src_ref=piece, dst_ref=piece, send_sem=send_x.at[peer, owner], recv_sem=recv_x.at[row, owner],
            device_id=(peer, gy), device_id_type=pl.DeviceIdType.MESH,
        )

    def unpack(row, owner):
        s = row * ngy + owner
        along_x, along_y = unpacked(held[row, owner, 1], width), unpacked(held[row, owner, 2], width)
        coarse[s, 0] = unpacked(held[row, owner, 0], width)
        coarse[s, 2] = along_x
        coarse[s, 4] = along_y

        @pl.when(row < ngx - 1)
        def _():
            coarse[s + ngy, 1] = along_x.T

        @pl.when(s < ngx * ngy - 1)
        def _():
            coarse[s + 1, 3] = along_y.T

    for d in range(1, ngy):
        over_y(gy, lax.rem(gy + d, ngy)).start()
    for d in range(1, ngx):
        over_x(gx, gy, lax.rem(gx + d, ngx)).start()
    for d in range(1, ngy):
        owner = lax.rem(gy + d, ngy)
        over_y(owner, owner).wait_recv()
        for e in range(1, ngx):
            over_x(gx, owner, lax.rem(gx + e, ngx)).start()

    @pl.loop(0, ngy)
    def _(owner):
        unpack(gx, owner)

    @pl.loop(0, ngy)
    def _(d):
        owner = lax.rem(gy + d, ngy)

        @pl.loop(1, ngx)
        def _(e):
            row = lax.rem(gx + e, ngx)
            over_x(row, owner, row).wait_recv()
            unpack(row, owner)

    for d in range(1, ngy):
        over_y(gy, lax.rem(gy + d, ngy)).wait_send()
    for d in range(ngy):
        owner = lax.rem(gy + d, ngy)
        for e in range(1, ngx):
            over_x(gx, owner, lax.rem(gx + e, ngx)).wait_send()


def spread(product, plus_x, plus_y):
    ngx, ngy = lax.axis_size("gx"), lax.axis_size("gy")
    width = plus_x.shape[0]
    vmem = pl.BlockSpec(memory_space=pltpu.VMEM)
    return pl.pallas_call(
        functools.partial(spread_kernel, ngx, ngy),
        in_specs=[vmem] * 3,
        out_specs=vmem,
        out_shape=jax.ShapeDtypeStruct((ngx * ngy, 5, width, width), jnp.float32),
        scratch_shapes=[
            pltpu.VMEM((ngx, ngy, 3, width * width // LANES, LANES), jnp.float32),
            pltpu.SemaphoreType.DMA((ngy,)),
            pltpu.SemaphoreType.DMA((ngy,)),
            pltpu.SemaphoreType.DMA((ngx, ngy)),
            pltpu.SemaphoreType.DMA((ngx, ngy)),
        ],
        compiler_params=pltpu.CompilerParams(collective_id=0, has_side_effects=True),
    )(product, plus_x, plus_y)


def on_device(basis, reaction):
    right_face = passed_along(basis[:, 0], "gx", -1)
    upper_face = passed_along(lower_face(basis), "gy", -1)
    phi, product, upper = extend(basis, reaction)
    plus_x = couple(basis[:, -1], right_face)
    plus_y = couple(upper, upper_face)
    return (phi, spread(product, plus_x, plus_y))


def solution(mesh):
    placed = (P(None, "gx", "gy", None), P("gx", "gy", None))
    return jax.shard_map(
        on_device,
        mesh=mesh,
        in_specs=placed,
        out_specs=(P(None, "gx", "gy", None), P()),
        check_vma=False,
    )
```

profile of v0, /device:TPU:0, one launch (start us, length us, event | category | flops | bytes accessed | tf_op | source)
XLA Modules:
  0.0 69.3 jit_solution(13807315031728467791)
XLA Ops:
  0.6 1.3 %slice_bitcast_fusion = (f32[32,16,256]{2,1,0:T(8,128)S(1)}, f32[32,1,16,256]{3,2,1,0:T(8,128)S(1)}) fusion(f32[32,16,16,256]{3,2,1,0:T(8,128)} %basis.3), kind=kLoop, calls=%fused_computation.5 | loop fusion | bytes 2097152 | tf_op jit(solution)/shard_map/squeeze | solution.py:320
  1.9 1.3 %collective-permute-start = (f32[32,16,256]{2,1,0:T(8,128)S(1)}, f32[32,16,256]{2,1,0:T(8,128)S(1)}, u32[]{:S(2)}, u32[]{:S(2)}) collective-permute-start(f32[32,16,256]{2,1,0:T(8,128)S(1)} %get-tuple-element.8), channel_id=1, source_target_pairs={{4,0},{8,4},{12,8},{16,12},{20,16},{24,20},{28,24},{5,1},{9,5},{13... | collective-permute-start | bytes 1572872 | tf_op jit(solution)/shard_map/ppermute | solution.py:19
  3.2 3.9 %shard_map.42 = f32[32,16,256]{2,1,0:T(8,128)} custom-call(f32[32,16,16,256]{3,2,1,0:T(8,128)} %basis.3), custom_call_target="tpu_custom_call" | custom-call | tf_op jit(solution)/shard_map/pallas_call | solution.py:177
  7.1 1.3 %collective-permute-start.1 = (f32[32,16,256]{2,1,0:T(8,128)}, f32[32,16,256]{2,1,0:T(8,128)S(1)}, u32[]{:S(2)}, u32[]{:S(2)}) collective-permute-start(f32[32,16,256]{2,1,0:T(8,128)} %shard_map.42), channel_id=1, source_target_pairs={{1,0},{2,1},{3,2},{5,4},{6,5},{7,6},{9,8},{10,9},{11,10},{13,12},{... | collective-permute-start | bytes 1572872 | tf_op jit(solution)/shard_map/ppermute | solution.py:19
  8.4 0.3 copy.6
  8.7 32.4 %shard_map.41 = (f32[32,16,16,256]{3,2,1,0:T(8,128)}, f32[64,64]{1,0:T(8,128)}, f32[32,16,256]{2,1,0:T(8,128)}) custom-call(f32[32,16,16,256]{3,2,1,0:T(8,128)} %basis.3, f32[16,16,256]{2,1,0:T(8,128)} %reaction.1), custom_call_target="tpu_custom_call" | custom-call | flops 125829120 | bytes 16777216 | tf_op jit(solution)/shard_map/pallas_call | solution.py:142
  41.1 0.0 collective-permute-done
  41.1 0.3 copy.7
  41.4 1.2 %convolution_negate_fusion.plus_x = f32[32,32]{1,0:T(8,128)} fusion(f32[32,4096]{1,0:T(8,128)S(1)} %bitcast.13, f32[32,4096]{1,0:T(8,128)S(1)} %bitcast.14), kind=kOutput, calls=%fused_computation.2 | convolution fusion | flops 50332672 | bytes 1052672 | tf_op jit(solution)/shard_map/dot_general | solution.py:188
  42.6 0.0 collective-permute-done.1
  42.6 2.7 %fusion.plus_y = f32[32,32]{1,0:T(8,128)} fusion(f32[32,16,256]{2,1,0:T(8,128)S(1)} %collective-permute-done.1, f32[32,16,256]{2,1,0:T(8,128)} %get-tuple-element.7), kind=kOutput, calls=%fused_computation.1 | convolution fusion | flops 50332672 | bytes 1052672 | tf_op jit(solution)/shard_map/dot_general | solution.py:188
  45.3 20.5 %shard_map.43 = f32[32,5,32,32]{3,2,1,0:T(8,128)} custom-call(f32[64,64]{1,0:T(8,128)} %get-tuple-element.6.product, f32[32,32]{1,0:T(8,128)} %convolution_negate_fusion.plus_x, f32[32,32]{1,0:T(8,128)} %fusion.plus_y), custom_call_target="tpu_custom_call" | custom-call | tf_op jit(solution)/shard_map/pallas_call | solution.py:303
  65.8 3.5 %copy.13 = f32[32,5,32,32]{3,2,1,0:T(8,128)} copy(f32[32,5,32,32]{3,2,1,0:T(8,128)} %shard_map.43) | data formatting | bytes 1310720
Async XLA Ops:
  1.9 39.2 %collective-permute-start = (f32[32,16,256]{2,1,0:T(8,128)S(1)}, f32[32,16,256]{2,1,0:T(8,128)S(1)}, u32[]{:S(2)}, u32[]{:S(2)}) collective-permute-start(f32[32,16,256]{2,1,0:T(8,128)S(1)} %get-tuple-element.8), channel_id=1, source_target_pairs={{4,0},{8,4},{12,8},{16,12},{20,16},{24,20},{28,24},{5,1},{9,5},{13... | collective-permute-start | bytes 1572872 | tf_op jit(solution)/shard_map/ppermute | solution.py:19
  7.1 35.5 %collective-permute-start.1 = (f32[32,16,256]{2,1,0:T(8,128)}, f32[32,16,256]{2,1,0:T(8,128)S(1)}, u32[]{:S(2)}, u32[]{:S(2)}) collective-permute-start(f32[32,16,256]{2,1,0:T(8,128)} %shard_map.42), channel_id=1, source_target_pairs={{1,0},{2,1},{3,2},{5,4},{6,5},{7,6},{9,8},{10,9},{11,10},{13,12},{... | collective-permute-start | bytes 1572872 | tf_op jit(solution)/shard_map/ppermute | solution.py:19
where the time goes:
time: 69.7 us; the launch traced here: 69.3 us
  Pallas kernels  56.8 us (81%)
  local copies, waits for them, and re-layouts  5.38 us (8%)
  matrix products  3.91 us (6%)
  starting transfers between devices  2.57 us (4%)
    pallas_call x1, Pallas kernels, extend(): pl.pallas_call(extend_kernel, grid=(width // GROUP,), in_specs=[block, pl...  32.4 us
    pallas_call x1, Pallas kernels, spread(): pl.pallas_call(functools.partial(spread_kernel, ngx, ngy), in_specs=[vmem...  20.5 us
    unnamed x3, local copies, waits for them, and re-layouts  4.1 us
    pallas_call x1, Pallas kernels, lower_face(): pl.pallas_call(face_kernel, grid=(width // GROUP,), in_specs=[pl.BlockSpe...  3.92 us
    dot_general x2, matrix products, couple(): jnp.dot(own.reshape(width, -1), other.reshape(width, -1).T, precision=lax...  3.91 us
    ppermute x2, starting transfers between devices, passed_along(): return lax.ppermute(block, axis, route)  2.57 us
  transfers between devices with their start and end apart: 2, of which 0 were waited for; matrix products, arithmetic and copies ran while one was open for 3% of the time, Pallas kernels for 52%

commit v1 on v0

v1 whole, which is shorter than its diff:
```python
import functools

import jax
import jax.numpy as jnp
from jax import lax
from jax.experimental import pallas as pl
from jax.experimental.pallas import tpu as pltpu
from jax.sharding import PartitionSpec as P

SWEEPS = 4
OMEGA = 0.8
ROWS = 8
LANES = 128
MESH = pl.DeviceIdType.MESH
F32 = jnp.float32
BF16 = jnp.bfloat16


def split(value):
    high = value.astype(BF16)
    low = (value - high.astype(F32)).astype(BF16)
    return high, low


def thirds(value):
    first = value.astype(BF16)
    rest = value - first.astype(F32)
    second = rest.astype(BF16)
    third = (rest - second.astype(F32)).astype(BF16)
    return jnp.concatenate([first, second, third], axis=0)


def block_sum(square, width):
    half = square.shape[0] // 2
    full = square[:half, :half] + square[:half, half:] + square[half:, :half]
    total = full[:width, :width]
    for i in range(width, half, width):
        total = total + full[i:i + width, i:i + width]
    return total


def packed(block):
    rows = block.shape[0] * block.shape[1] // LANES
    return jnp.concatenate(
        [block[i:i + rows] for i in range(0, block.shape[0], rows)], axis=1
    )


def unpacked(tile, width):
    return jnp.concatenate(
        [tile[:, i:i + width] for i in range(0, LANES, width)], axis=0
    )


def main_kernel(
    ngx, ngy, basis, reaction, nat, tiles,
    react, spread, weight, centre, first, second, left0, left1, right0, right1,
    gram, face_x, face_y, held,
    in_sem, react_sem, face_send, face_recv, send_y, recv_y, send_x, recv_x,
):
    width, cx, cy, cz = basis.shape
    yo = LANES // width
    yi = cy // yo
    group = cx // yo
    halves = cz // LANES
    ztiles = cz // ROWS
    gx, gy = lax.axis_index("gx"), lax.axis_index("gy")

    barrier = pltpu.get_barrier_semaphore()
    for d in range(1, ngy):
        pl.semaphore_signal(barrier, inc=1, device_id=(gx, lax.rem(gy + d, ngy)), device_id_type=MESH)
    for d in range(1, ngx):
        pl.semaphore_signal(barrier, inc=1, device_id=(lax.rem(gx + d, ngx), gy), device_id_type=MESH)

    load = pltpu.make_async_copy(reaction, react, react_sem)
    load.start()

    @pl.loop(0, cx)
    def _(x):
        for y in range(cy):
            pltpu.make_async_copy(
                basis.at[:, x, y, :],
                nat.at[x, y % yi, pl.ds((y // yi) * width, width), :],
                in_sem.at[x],
            ).start()

    def arrived(x):
        pltpu.make_async_copy(nat.at[x], nat.at[x], in_sem.at[x]).wait()

    def over_x(peer):
        return pltpu.make_async_remote_copy(
            src_ref=nat.at[0], dst_ref=face_x, send_sem=face_send.at[0], recv_sem=face_recv.at[0],
            device_id=(peer, gy), device_id_type=MESH,
        )

    def over_y(x, peer):
        return pltpu.make_async_remote_copy(
            src_ref=nat.at[x, 0, pl.ds(0, width), :],
            dst_ref=face_y.at[x // yo, pl.ds(lax.rem(x, yo) * width, width), :],
            send_sem=face_send.at[1], recv_sem=face_recv.at[1],
            device_id=(gx, peer), device_id_type=MESH,
        )

    rows = lax.broadcasted_iota(jnp.int32, (cy, yi * LANES), 0)
    cols = lax.broadcasted_iota(jnp.int32, (cy, yi * LANES), 1)
    chosen = rows == (lax.rem(cols, LANES) // width) * yi + cols // LANES
    pick = jnp.where(chosen, 1.0, 0.0).astype(BF16)
    spread[...] = jnp.concatenate([pick, pick, pick], axis=0)

    blank = jnp.zeros((ROWS, LANES), F32)
    for buffer in (first, second):
        @pl.loop(0, cx)
        def _(x):
            for j in range(yi):
                buffer[x, j, 0:ROWS, :] = blank
                buffer[x, j, cz + ROWS:cz + 2 * ROWS, :] = blank

    left1[...] = jnp.zeros_like(left1)
    right1[...] = jnp.zeros_like(right1)
    gram[...] = jnp.zeros_like(gram)

    def expanded(values):
        return lax.dot_general(
            thirds(values), spread[...], (((0,), (0,)), ((), ())), preferred_element_type=F32
        )

    load.wait()
    line = lax.broadcasted_iota(jnp.int32, (cy, cz), 0)
    face_row = (line == 0) | (line == cy - 1)

    @pl.loop(1, cx - 1)
    def _(x):
        scaled = jnp.where(face_row, 0.0, OMEGA / (6.0 + react[x]))
        wide = expanded(scaled)
        for j in range(yi):
            weight[x, j] = wide[:, j * LANES:(j + 1) * LANES]

    pl.semaphore_wait(barrier, ngx + ngy - 2)

    lane = lax.broadcasted_iota(jnp.int32, (ROWS, LANES), 1)
    keep = [jnp.full((ROWS, LANES), 1.0 - OMEGA, F32) for _ in range(yi)]
    keep[0] = jnp.where(lane < width, 1.0, keep[0])
    keep[yi - 1] = jnp.where(lane >= LANES - width, 1.0, keep[yi - 1])

    def take_in(x):
        arrived(x)

        @pl.when(gy > 0)
        def _():
            over_y(x, gy - 1).start()

        for j in range(yi):
            for h in range(halves):
                part = nat[x, j, :, h * LANES:(h + 1) * LANES]
                first[x, j, ROWS + h * LANES:ROWS + (h + 1) * LANES, :] = part.T

    def line_of(ref, x, t, shift=0):
        return [ref[x, j, pl.ds(ROWS + t * ROWS + shift, ROWS), :] for j in range(yi)]

    def ring(values):
        before = pltpu.roll(values[yi - 1], width, 1)
        after = pltpu.roll(values[0], LANES - width, 1)
        return [before] + values + [after]

    def update(source, target, x, t, down, here, up):
        near = ring(here)
        below, above = line_of(source, x, t, -1), line_of(source, x, t, 1)
        out = []
        for j in range(yi):
            total = (down[j] + up[j]) + (near[j] + near[j + 2]) + (below[j] + above[j])
            value = keep[j] * here[j] + weight[x, j, pl.ds(t * ROWS, ROWS), :] * total
            target[x, j, pl.ds(ROWS + t * ROWS, ROWS), :] = value
            out.append(value)
        return out

    def sweep_row(source, target, x):
        for t in range(ztiles):
            update(
                source, target, x, t,
                line_of(source, x - 1, t), line_of(source, x, t), line_of(source, x + 1, t),
            )

    def sweep(source, target):
        @pl.loop(0, ztiles, unroll=2)
        def _(t):
            down, here = line_of(source, 0, t), line_of(source, 1, t)
            for x in range(1, cx - 1):
                up = line_of(source, x + 1, t)
                update(source, target, x, t, down, here, up)
                down, here = here, up

    take_in(0)

    @pl.when(gx > 0)
    def _():
        over_x(gx - 1).start()

    take_in(1)
    take_in(2)

    @pl.loop(3, cx)
    def _(x):
        take_in(x)
        sweep_row(first, second, x - 2)

    sweep_row(first, second, cx - 2)

    @pl.loop(0, ztiles)
    def _(t):
        for x in (0, cx - 1):
            for j, value in enumerate(line_of(first, x, t)):
                second[x, j, pl.ds(ROWS + t * ROWS, ROWS), :] = value

    sweep(second, first)
    sweep(first, second)

    def couple():
        return -block_sum(
            lax.dot_general(
                left0[...], left1[...], (((1,), (1,)), ((), ())), preferred_element_type=F32
            ),
            width,
        )

    def fill(ref, row, column, value):
        high, low = split(value)
        size = value.shape[0]
        ref[row:row + size, column * cz:(column + 1) * cz] = high
        ref[LANES + row:LANES + row + size, column * cz:(column + 1) * cz] = low

    @pl.when(gx < ngx - 1)
    def _():
        over_x(gx).wait_recv()

    for j in range(yi):
        fill(left0, 0, j, nat[cx - 1, j])
        fill(left1, 0, j, face_x[j])
    plus_x = couple()
    held[gx, gy, 1] = packed(plus_x)
    held[gx, gy, 2] = packed(plus_x.T)

    @pl.when(gy < ngy - 1)
    def _():
        pltpu.make_async_copy(face_y, face_y, face_recv.at[1]).wait()

    for x in range(cx):
        fill(left0, (x % yo) * width, x // yo, nat[x, yi - 1, LANES - width:, :])
    for j in range(group):
        fill(left1, 0, j, face_y[j])
    plus_y = couple()
    held[gx, gy, 3] = packed(plus_y)
    held[gx, gy, 4] = packed(plus_y.T)

    @pl.when(gx > 0)
    def _():
        over_x(gx).wait_send()

    @pl.when(gy > 0)
    def _():
        pltpu.make_async_copy(face_y, face_y, face_send.at[1]).wait()

    left1[...] = jnp.zeros_like(left1)

    def product(x, left, right, last=False):
        wide = expanded(3.0 + 0.5 * react[x])
        for j in range(yi):
            centre[j] = wide[:, j * LANES:(j + 1) * LANES]
        for t in range(ztiles):
            here = line_of(second_out, x, t)
            above = line_of(second_out, x, t, 1)
            up = None if last else line_of(second_out, x + 1, t)
            edge = jnp.where(
                lane >= LANES - width, 0.0, pltpu.roll(here[0], LANES - width, 1)
            )
            beside = here[1:] + [edge]
            for j in range(yi):
                total = beside[j] + above[j]
                if up is not None:
                    total = total + up[j]
                applied = centre[j, t * ROWS:(t + 1) * ROWS, :] * here[j] - total
                work[j, t * ROWS:(t + 1) * ROWS, :] = applied
        for j in range(yi):
            high, low = split(work[j])
            right[j * cz:(j + 1) * cz, :LANES] = high
            right[j * cz:(j + 1) * cz, LANES:] = low
            for h in range(halves):
                part = second_out[x, j, ROWS + h * LANES:ROWS + (h + 1) * LANES, :].T
                nat[x, j, :, h * LANES:(h + 1) * LANES] = part
                high, low = split(part)
                left[:LANES, j * cz + h * LANES:j * cz + (h + 1) * LANES] = high
                left[LANES:, j * cz + h * LANES:j * cz + (h + 1) * LANES] = low

    def gather_product(left, right):
        gram[...] += jnp.dot(left[...], right[...], preferred_element_type=F32)

    source, second_out = second, first
    work = centre

    @pl.loop(0, cx - 2, step=2)
    def _(x):
        gather_product(left1, right1)
        sweep_row(source, second_out, x + 1)
        product(x, left0, right0)
        gather_product(left0, right0)
        sweep_row(source, second_out, x + 2)
        product(x + 1, left1, right1)

    gather_product(left1, right1)
    product(cx - 2, left0, right0)
    gather_product(left0, right0)
    product(cx - 1, left1, right1, last=True)
    gather_product(left1, right1)

    half = block_sum(gram[...], width)
    held[gx, gy, 0] = packed(half + half.T)

    def to_y(owner, peer):
        piece = held.at[gx, owner]
        return pltpu.make_async_remote_copy(
            src_ref=piece, dst_ref=piece, send_sem=send_y.at[peer], recv_sem=recv_y.at[owner],
            device_id=(gx, peer), device_id_type=MESH,
        )

    def to_x(row, owner, peer):
        piece = held.at[row, owner]
        return pltpu.make_async_remote_copy(
            src_ref=piece, dst_ref=piece, send_sem=send_x.at[peer, owner], recv_sem=recv_x.at[row, owner],
            device_id=(peer, gy), device_id_type=MESH,
        )

    for d in range(1, ngy):
        to_y(gy, lax.rem(gy + d, ngy)).start()
    for d in range(1, ngx):
        to_x(gx, gy, lax.rem(gx + d, ngx)).start()
    for d in range(1, ngy):
        owner = lax.rem(gy + d, ngy)
        to_y(owner, owner).wait_recv()
        for e in range(1, ngx):
            to_x(gx, owner, lax.rem(gx + e, ngx)).start()
    for d in range(ngy):
        owner = lax.rem(gy + d, ngy)
        for e in range(1, ngx):
            row = lax.rem(gx + e, ngx)
            to_x(row, owner, row).wait_recv()
    for d in range(1, ngy):
        to_y(gy, lax.rem(gy + d, ngy)).wait_send()
    for d in range(ngy):
        owner = lax.rem(gy + d, ngy)
        for e in range(1, ngx):
            to_x(gx, owner, lax.rem(gx + e, ngx)).wait_send()
    tiles[...] = held[...]


def main(basis, reaction):
    ngx, ngy = lax.axis_size("gx"), lax.axis_size("gy")
    width, cx, cy, cz = basis.shape
    yo = LANES // width
    yi = cy // yo
    hbm = pl.BlockSpec(memory_space=pltpu.HBM)
    vmem = pl.BlockSpec(memory_space=pltpu.VMEM)
    field = pltpu.VMEM((cx, yi, cz + 2 * ROWS, LANES), F32)
    left = pltpu.VMEM((2 * LANES, yi * cz), BF16)
    right = pltpu.VMEM((yi * cz, 2 * LANES), BF16)
    held = (ngx, ngy, 5, width * width // LANES, LANES)
    return pl.pallas_call(
        functools.partial(main_kernel, ngx, ngy),
        in_specs=[hbm, hbm],
        out_specs=[vmem, vmem],
        out_shape=[
            jax.ShapeDtypeStruct((cx, yi, LANES, cz), F32),
            jax.ShapeDtypeStruct(held, F32),
        ],
        scratch_shapes=[
            pltpu.VMEM((cx, cy, cz), F32),
            pltpu.VMEM((3 * cy, yi * LANES), BF16),
            pltpu.VMEM((cx, yi, cz, LANES), F32),
            pltpu.VMEM((yi, cz, LANES), F32),
            field, field, left, left, right, right,
            pltpu.VMEM((2 * LANES, 2 * LANES), F32),
            pltpu.VMEM((yi, LANES, cz), F32),
            pltpu.VMEM((cx // yo, LANES, cz), F32),
            pltpu.VMEM(held, F32),
            pltpu.SemaphoreType.DMA((cx,)),
            pltpu.SemaphoreType.DMA,
            pltpu.SemaphoreType.DMA((2,)),
            pltpu.SemaphoreType.DMA((2,)),
            pltpu.SemaphoreType.DMA((ngy,)),
            pltpu.SemaphoreType.DMA((ngy,)),
            pltpu.SemaphoreType.DMA((ngx, ngy)),
            pltpu.SemaphoreType.DMA((ngx, ngy)),
        ],
        compiler_params=pltpu.CompilerParams(
            collective_id=0, has_side_effects=True, vmem_limit_bytes=48 * 2**20
        ),
        cost_estimate=pl.CostEstimate(
            flops=60 * basis.size, bytes_accessed=8 * basis.size, transcendentals=0
        ),
    )(basis, reaction)


def write_kernel(nat, tiles, extended, coarse, blocks, out_sem, coarse_sem):
    width, cx, cy, cz = extended.shape
    ngx, ngy = tiles.shape[:2]
    yi = nat.shape[1]

    @pl.loop(0, cx)
    def _(x):
        for y in range(cy):
            pltpu.make_async_copy(
                nat.at[x, y % yi, pl.ds((y // yi) * width, width), :],
                extended.at[:, x, y, :],
                out_sem.at[x],
            ).start()

    nothing = jnp.zeros((width, width), F32)

    @pl.loop(0, ngx)
    def _(row):
        for col in range(ngy):
            s = row * ngy + col
            below, above = jnp.maximum(row - 1, 0), row
            blocks[s, 0] = unpacked(tiles[row, col, 0], width)
            blocks[s, 1] = jnp.where(row > 0, unpacked(tiles[below, col, 2], width), 0.0)
            blocks[s, 2] = jnp.where(row < ngx - 1, unpacked(tiles[above, col, 1], width), 0.0)
            blocks[s, 3] = unpacked(tiles[row, col - 1, 4], width) if col > 0 else nothing
            blocks[s, 4] = unpacked(tiles[row, col, 3], width) if col < ngy - 1 else nothing

    copy = pltpu.make_async_copy(blocks, coarse, coarse_sem)
    copy.start()

    @pl.loop(0, cx)
    def _(x):
        pltpu.make_async_copy(nat.at[x], nat.at[x], out_sem.at[x]).wait()

    copy.wait()


def write(nat, tiles, shape):
    width, cx, cy, cz = shape
    ngx, ngy = tiles.shape[:2]
    vmem = pl.BlockSpec(memory_space=pltpu.VMEM)
    hbm = pl.BlockSpec(memory_space=pltpu.HBM)
    coarse = (ngx * ngy, 5, width, width)
    return pl.pallas_call(
        write_kernel,
        in_specs=[vmem, vmem],
        out_specs=[hbm, hbm],
        out_shape=[jax.ShapeDtypeStruct(shape, F32), jax.ShapeDtypeStruct(coarse, F32)],
        scratch_shapes=[
            pltpu.VMEM(coarse, F32),
            pltpu.SemaphoreType.DMA((cx,)),
            pltpu.SemaphoreType.DMA,
        ],
        compiler_params=pltpu.CompilerParams(vmem_limit_bytes=16 * 2**20),
    )(nat, tiles)


def on_device(basis, reaction):
    nat, tiles = main(basis, reaction)
    extended, coarse = write(nat, tiles, basis.shape)
    return extended, coarse


def solution(mesh):
    placed = (P(None, "gx", "gy", None), P("gx", "gy", None))
    return jax.shard_map(
        on_device,
        mesh=mesh,
        in_specs=placed,
        out_specs=(P(None, "gx", "gy", None), P()),
        check_vma=False,
    )
```

time: 69.7 us -> 55 us (0.79)
  Pallas kernels: 56.8 us -> 49.8 us
  matrix products: 3.91 us -> 0 us
  starting transfers between devices: 2.57 us -> 0 us
  local copies, waits for them, and re-layouts: 5.38 us -> 4.32 us
    pallas_call x3 -> x2, Pallas kernels: 56.8 us -> 49.8 us  [the longest x1 45.6 us: main(): pl.pallas_call(functools.partial(main_kernel, ngx, ngy), in_specs=[hbm, h...]
    dot_general x2 -> x0, matrix products: 3.91 us -> none  [couple(): jnp.dot(own.reshape(width, -1), other.reshape(width, -1).T, precision=lax...]
    ppermute x2 -> x0, starting transfers between devices: 2.57 us -> none  [passed_along(): return lax.ppermute(block, axis, route)]
    squeeze x1 -> x0, local copies, waits for them, and re-layouts: 1.28 us -> none  [on_device(): right_face = passed_along(basis[:, 0], 'gx', -1)]
    unnamed x3 -> x4, local copies, waits for them, and re-layouts: 4.1 us -> 4.32 us
  transfers between devices with their start and end apart: 2 -> 0, of which waited for: 0 -> 0; matrix products, arithmetic and copies ran while one was open for 3% -> 0% of each run, Pallas kernels for 52% -> 0%
where the time goes in v1:
time: 55 us; the launch traced here: 54.8 us
  Pallas kernels  49.8 us (91%)
  local copies, waits for them, and re-layouts  4.32 us (8%)
  between operations  0.65 us (1%)
    pallas_call x1, Pallas kernels, main(): pl.pallas_call(functools.partial(main_kernel, ngx, ngy), in_specs=[hbm, h...  45.6 us
    unnamed x4, local copies, waits for them, and re-layouts  4.32 us
    pallas_call x1, Pallas kernels, write(): pl.pallas_call(write_kernel, in_specs=[vmem, vmem], out_specs=[hbm, hbm],...  4.2 us

profile of v1, /device:TPU:0, one launch (start us, length us, event | category | flops | bytes accessed | tf_op | source)
XLA Modules:
  0.0 54.8 jit_solution(13529646231252339986)
XLA Ops:
  0.6 0.0 copy-start.1
  0.6 0.9 %copy-done.1 = f32[16,16,256]{2,1,0:T(8,128)S(1)} copy-done((f32[16,16,256]{2,1,0:T(8,128)S(1)}, f32[16,16,256]{2,1,0:T(8,128)}, u32[]{:S(2)}) %copy-start.1) | copy-done | bytes 262168
  1.6 45.6 %shard_map.41 = (f32[16,4,128,256]{3,2,1,0:T(8,128)}, f32[8,4,5,8,128]{4,3,2,1,0:T(8,128)S(1)}) custom-call(f32[32,16,16,256]{3,2,1,0:T(8,128)} %basis.1, f32[16,16,256]{2,1,0:T(8,128)S(1)} %copy-done.1), custom_call_target="tpu_custom_call" | custom-call | flops 125829120 | bytes 16777216 | tf_op jit(solution)/shard_map/pallas_call | solution.py:365
  47.2 0.0 copy-start
  47.2 3.4 %copy-done = f32[16,4,128,256]{3,2,1,0:T(8,128)S(1)} copy-done((f32[16,4,128,256]{3,2,1,0:T(8,128)S(1)}, f32[16,4,128,256]{3,2,1,0:T(8,128)}, u32[]{:S(2)}) %copy-start) | copy-done | bytes 8388632
  50.6 4.2 %shard_map.42 = (f32[32,16,16,256]{3,2,1,0:T(8,128)}, f32[32,5,32,32]{3,2,1,0:T(8,128)}) custom-call(f32[16,4,128,256]{3,2,1,0:T(8,128)S(1)} %copy-done, f32[8,4,5,8,128]{4,3,2,1,0:T(8,128)S(1)} %get-tuple-element.5.tiles), custom_call_target="tpu_custom_call" | custom-call | tf_op jit(solution)/shard_map/pallas_call | solution.py:444
Async XLA Ops:
  0.6 1.0 %copy-start.1 = (f32[16,16,256]{2,1,0:T(8,128)S(1)}, f32[16,16,256]{2,1,0:T(8,128)}, u32[]{:S(2)}) copy-start(f32[16,16,256]{2,1,0:T(8,128)} %reaction.1) | copy-start | bytes 786436
  47.2 3.4 %copy-start = (f32[16,4,128,256]{3,2,1,0:T(8,128)S(1)}, f32[16,4,128,256]{3,2,1,0:T(8,128)}, u32[]{:S(2)}) copy-start(f32[16,4,128,256]{3,2,1,0:T(8,128)} %get-tuple-element.4.nat) | copy-start | bytes 25165828

commit v2 on v1

v2 whole, which is shorter than its diff:
```python
import functools

import jax
import jax.numpy as jnp
from jax import lax
from jax.experimental import pallas as pl
from jax.experimental.pallas import tpu as pltpu
from jax.sharding import PartitionSpec as P

SWEEPS = 4
OMEGA = 0.8
ROWS = 8
LANES = 128
MESH = pl.DeviceIdType.MESH
F32 = jnp.float32
BF16 = jnp.bfloat16


def split(value):
    high = value.astype(BF16)
    low = (value - high.astype(F32)).astype(BF16)
    return high, low


def thirds(value):
    first = value.astype(BF16)
    rest = value - first.astype(F32)
    second = rest.astype(BF16)
    third = (rest - second.astype(F32)).astype(BF16)
    return jnp.concatenate([first, second, third], axis=0)


def block_sum(square, width):
    half = square.shape[0] // 2
    full = square[:half, :half] + square[:half, half:] + square[half:, :half]
    total = full[:width, :width]
    for i in range(width, half, width):
        total = total + full[i:i + width, i:i + width]
    return total


def packed(block):
    rows = block.shape[0] * block.shape[1] // LANES
    return jnp.concatenate(
        [block[i:i + rows] for i in range(0, block.shape[0], rows)], axis=1
    )


def unpacked(tile, width):
    return jnp.concatenate(
        [tile[:, i:i + width] for i in range(0, LANES, width)], axis=0
    )


def main_kernel(
    ngx, ngy, basis, reaction, nat, tiles,
    react, spread, weight, centre, first, second, lefts, rights,
    gram, face_x, face_y, pairs, diag,
    in_sem, react_sem, face_send, face_recv,
    pair_send_y, pair_recv_y, pair_send_x, pair_recv_x,
    diag_send_y, diag_recv_y, diag_send_x, diag_recv_x,
):
    width, cx, cy, cz = basis.shape
    yo = LANES // width
    yi = cy // yo
    group = cx // yo
    halves = cz // LANES
    ztiles = cz // ROWS
    gx, gy = lax.axis_index("gx"), lax.axis_index("gy")

    barrier = pltpu.get_barrier_semaphore()
    for d in range(1, ngy):
        pl.semaphore_signal(barrier, inc=1, device_id=(gx, lax.rem(gy + d, ngy)), device_id_type=MESH)
    for d in range(1, ngx):
        pl.semaphore_signal(barrier, inc=1, device_id=(lax.rem(gx + d, ngx), gy), device_id_type=MESH)

    load = pltpu.make_async_copy(reaction, react, react_sem)
    load.start()

    def bring(x):
        for y in range(cy):
            pltpu.make_async_copy(
                basis.at[:, x, y, :],
                nat.at[x, y % yi, pl.ds((y // yi) * width, width), :],
                in_sem.at[x],
            ).start()

    bring(0)

    def over_x(peer):
        return pltpu.make_async_remote_copy(
            src_ref=nat.at[0], dst_ref=face_x, send_sem=face_send.at[0], recv_sem=face_recv.at[0],
            device_id=(peer, gy), device_id_type=MESH,
        )

    def over_y(x, upper, peer):
        plane, start = (yi - 1, LANES - width) if upper else (0, 0)
        return pltpu.make_async_remote_copy(
            src_ref=nat.at[x, plane, pl.ds(start, width), :],
            dst_ref=face_y.at[x // yo, pl.ds(lax.rem(x, yo) * width, width), :],
            send_sem=face_send.at[1 + upper], recv_sem=face_recv.at[1 + upper],
            device_id=(gx, peer), device_id_type=MESH,
        )

    middle = (group // 2) * yo

    rows = lax.broadcasted_iota(jnp.int32, (cy, yi * LANES), 0)
    cols = lax.broadcasted_iota(jnp.int32, (cy, yi * LANES), 1)
    chosen = rows == (lax.rem(cols, LANES) // width) * yi + cols // LANES
    pick = jnp.where(chosen, 1.0, 0.0).astype(BF16)
    spread[...] = jnp.concatenate([pick, pick, pick], axis=0)

    def expanded(values):
        return lax.dot_general(
            thirds(values), spread[...], (((0,), (0,)), ((), ())), preferred_element_type=F32
        )

    line = lax.broadcasted_iota(jnp.int32, (cy, cz), 0)
    face_row = (line == 0) | (line == cy - 1)
    blank = jnp.zeros((ROWS, LANES), F32)
    load.wait()

    @pl.loop(1, cx)
    def _(x):
        bring(x)
        scaled = jnp.where(face_row, 0.0, OMEGA / (6.0 + react[x]))
        wide = expanded(scaled)
        for j in range(yi):
            weight[x, j] = wide[:, j * LANES:(j + 1) * LANES]
            for buffer in (first, second):
                buffer[x, j, 0:ROWS, :] = blank
                buffer[x, j, cz + ROWS:cz + 2 * ROWS, :] = blank

    for j in range(yi):
        for buffer in (first, second):
            buffer[0, j, 0:ROWS, :] = blank
            buffer[0, j, cz + ROWS:cz + 2 * ROWS, :] = blank
    gram[...] = jnp.zeros_like(gram)

    pl.semaphore_wait(barrier, ngx + ngy - 2)

    lane = lax.broadcasted_iota(jnp.int32, (ROWS, LANES), 1)
    keep = [jnp.full((ROWS, LANES), 1.0 - OMEGA, F32) for _ in range(yi)]
    keep[0] = jnp.where(lane < width, 1.0, keep[0])
    keep[yi - 1] = jnp.where(lane >= LANES - width, 1.0, keep[yi - 1])

    def land(x):
        pltpu.make_async_copy(nat.at[x], nat.at[x], in_sem.at[x]).wait()

        @pl.when((x < middle) & (gy > 0))
        def _():
            over_y(x, 0, gy - 1).start()

        @pl.when((x >= middle) & (gy < ngy - 1))
        def _():
            over_y(x, 1, gy + 1).start()

    def take_in(x, j, h):
        part = nat[x, j, :, h * LANES:(h + 1) * LANES]
        first[x, j, ROWS + h * LANES:ROWS + (h + 1) * LANES, :] = part.T

    squares = [(j, h) for j in range(yi) for h in range(halves)]

    def line_of(ref, x, t, shift=0):
        return [ref[x, j, pl.ds(ROWS + t * ROWS + shift, ROWS), :] for j in range(yi)]

    def forward(values):
        return pltpu.roll(values[0], LANES - width, 1)

    def backward(values):
        return pltpu.roll(values[yi - 1], width, 1)

    def diagonals(here, up):
        inner = [here[j] + up[j + 1] for j in range(yi - 1)]
        return [backward(here) + up[0]] + inner + [here[yi - 1] + forward(up)]

    def finish(source, target, x, t, here, total):
        below, above = line_of(source, x, t, -1), line_of(source, x, t, 1)
        for j in range(yi):
            around = total[j] + (below[j] + above[j])
            target[x, j, pl.ds(ROWS + t * ROWS, ROWS), :] = (
                keep[j] * here[j] + weight[x, j, pl.ds(t * ROWS, ROWS), :] * around
            )

    def sweep_pair(source, target, x, t):
        field = [line_of(source, x + i, t) for i in range(4)]
        for i in range(1, 3):
            down, here, up = field[i - 1:i + 2]
            near = [backward(here)] + here + [forward(here)]
            total = [(down[j] + up[j]) + (near[j] + near[j + 2]) for j in range(yi)]
            finish(source, target, x + i, t, here, total)

    def sweep(source, target):
        @pl.loop(0, ztiles, unroll=2)
        def _(t):
            here = line_of(source, 1, t)
            old = diagonals(line_of(source, 0, t), here)
            for x in range(1, cx - 1):
                up = line_of(source, x + 1, t)
                new = diagonals(here, up)
                total = [old[j + 1] + new[j] for j in range(yi)]
                finish(source, target, x, t, here, total)
                old, here = new, up

    land(0)

    @pl.when(gx > 0)
    def _():
        over_x(gx - 1).start()

    for x in range(4):
        if x:
            land(x)
        for square in squares:
            take_in(x, *square)

    each = ztiles // (2 * len(squares))

    @pl.loop(0, cx - 4, step=2)
    def _(x):
        land(x + 4)
        land(x + 5)
        for i in range(2):
            for n, square in enumerate(squares):
                take_in(x + 4 + i, *square)
                for m in range(each):
                    sweep_pair(first, second, x, (i * len(squares) + n) * each + m)

    for t in range(ztiles):
        sweep_pair(first, second, cx - 4, t)

    @pl.loop(0, ztiles)
    def _(t):
        for x in (0, cx - 1):
            for j, value in enumerate(line_of(first, x, t)):
                second[x, j, pl.ds(ROWS + t * ROWS, ROWS), :] = value

    sweep(second, first)
    sweep(first, second)

    def joined(ref, start=0, stop=None):
        stop = ref.shape[0] if stop is None else stop
        return jnp.concatenate([ref[i] for i in range(start, stop)], axis=1)

    def couple(start, stop):
        return -block_sum(
            lax.dot_general(
                joined(lefts.at[0], start, stop), joined(lefts.at[1], start, stop),
                (((1,), (1,)), ((), ())), preferred_element_type=F32,
            ),
            width,
        )

    def fill(ref, row, column, value):
        size = value.shape[0]
        for h in range(halves):
            high, low = split(value[:, h * LANES:(h + 1) * LANES])
            ref[column * halves + h, row:row + size] = high
            ref[column * halves + h, LANES + row:LANES + row + size] = low

    @pl.when(gx < ngx - 1)
    def _():
        over_x(gx).wait_recv()

    for j in range(yi):
        fill(lefts.at[0], 0, j, nat[cx - 1, j])
        fill(lefts.at[1], 0, j, face_x[j])
    pairs[gx, gy, 0] = packed(couple(0, yi * halves))

    near, far = face_y.at[pl.ds(0, group // 2)], face_y.at[pl.ds(group // 2, group - group // 2)]

    @pl.when(gy < ngy - 1)
    def _():
        pltpu.make_async_copy(near, near, face_recv.at[1]).wait()

    @pl.when(gy > 0)
    def _():
        pltpu.make_async_copy(far, far, face_recv.at[2]).wait()

    for x in range(cx):
        own = nat[x, yi - 1, LANES - width:, :] if x < middle else nat[x, 0, :width, :]
        fill(lefts.at[0 if x < middle else 1], (x % yo) * width, x // yo, own)
    for j in range(group):
        fill(lefts.at[1 if j < group // 2 else 0], 0, j, face_y[j])
    pairs[gx, gy, 1] = packed(couple(0, (group // 2) * halves))
    pairs[gx, gy, 2] = packed(couple((group // 2) * halves, group * halves))

    @pl.when(gx > 0)
    def _():
        over_x(gx).wait_send()

    @pl.when(gy > 0)
    def _():
        pltpu.make_async_copy(near, near, face_send.at[1]).wait()

    @pl.when(gy < ngy - 1)
    def _():
        pltpu.make_async_copy(far, far, face_send.at[2]).wait()

    def to_y(ref, send, recv, owner, peer):
        piece = ref.at[gx, owner]
        return pltpu.make_async_remote_copy(
            src_ref=piece, dst_ref=piece, send_sem=send.at[peer], recv_sem=recv.at[owner],
            device_id=(gx, peer), device_id_type=MESH,
        )

    def to_x(ref, send, recv, row, owner, peer):
        piece = ref.at[row, owner]
        return pltpu.make_async_remote_copy(
            src_ref=piece, dst_ref=piece, send_sem=send.at[peer, owner], recv_sem=recv.at[row, owner],
            device_id=(peer, gy), device_id_type=MESH,
        )

    ys = [lax.rem(gy + d, ngy) for d in range(1, ngy)]
    xs = [lax.rem(gx + d, ngx) for d in range(1, ngx)]

    def gather_start(ref, send_y, recv_y, send_x, recv_x):
        for peer in ys:
            to_y(ref, send_y, recv_y, gy, peer).start()
        for peer in xs:
            to_x(ref, send_x, recv_x, gx, gy, peer).start()

    def gather_pass(ref, send_y, recv_y, send_x, recv_x):
        for owner in ys:
            to_y(ref, send_y, recv_y, owner, owner).wait_recv()
            for peer in xs:
                to_x(ref, send_x, recv_x, gx, owner, peer).start()

    def gather_end(ref, send_y, recv_y, send_x, recv_x):
        for owner in [gy] + ys:
            for row in xs:
                to_x(ref, send_x, recv_x, row, owner, row).wait_recv()
        for peer in ys:
            to_y(ref, send_y, recv_y, gy, peer).wait_send()
        for owner in [gy] + ys:
            for peer in xs:
                to_x(ref, send_x, recv_x, gx, owner, peer).wait_send()

    pair_way = (pairs, pair_send_y, pair_recv_y, pair_send_x, pair_recv_x)
    diag_way = (diag, diag_send_y, diag_recv_y, diag_send_x, diag_recv_x)
    gather_start(*pair_way)

    source, result = second, first

    def applied(x, i, slot, t, last):
        here, above = line_of(result, x, t), line_of(result, x, t, 1)
        up = None if last else line_of(result, x + 1, t)
        edge = jnp.where(lane >= LANES - width, 0.0, forward(here))
        beside = here[1:] + [edge]
        out = []
        for j in range(yi):
            total = beside[j] + above[j]
            if up is not None:
                total = total + up[j]
            out.append(centre[slot + i, j, t * ROWS:(t + 1) * ROWS, :] * here[j] - total)
        return out

    def block(x, slot, sweeping=True, last=False):
        for i in range(2):
            wide = expanded(3.0 + 0.5 * react[x + i])
            for j in range(yi):
                centre[slot + i, j] = wide[:, j * LANES:(j + 1) * LANES]
        for n in range(ztiles // 2):
            if sweeping:
                for t in (2 * n, 2 * n + 1):
                    sweep_pair(source, result, x + 2, t)
            for i in range(2):
                two = [applied(x + i, i, slot, t, last and i == 1) for t in (2 * n, 2 * n + 1)]
                for j in range(yi):
                    at = j * cz + n * 2 * ROWS
                    both = jnp.concatenate([two[0][j], two[1][j]], axis=0)
                    for part, value in enumerate(split(both)):
                        rights[slot + i, part, at:at + 2 * ROWS] = value
            i, (j, h) = n // len(squares), squares[n % len(squares)]
            part = result[x + i, j, ROWS + h * LANES:ROWS + (h + 1) * LANES, :].T
            nat[x + i, j, :, h * LANES:(h + 1) * LANES] = part
            for half, value in enumerate(split(part)):
                lefts[slot + i, j * halves + h, half * LANES:(half + 1) * LANES] = value

    def multiply(slot, fresh=None):
        for i in range(2):
            total = gram[...] + jnp.dot(
                joined(lefts.at[slot + i]), joined(rights.at[slot + i]), preferred_element_type=F32
            )
            gram[...] = total if fresh is None else jnp.where(fresh, 0.0, total)

    for t in range(ztiles):
        sweep_pair(source, result, 0, t)

    steps = (cx - 4) // 4

    @pl.loop(0, steps)
    def _(n):
        @pl.when(n == steps - 1)
        def _():
            gather_pass(*pair_way)

        multiply(2, n == 0)
        block(4 * n, 0)
        multiply(0)
        block(4 * n + 2, 2)

    multiply(2)
    block(cx - 4, 0, sweeping=False)
    multiply(0)
    block(cx - 2, 2, sweeping=False, last=True)
    multiply(2)

    half = block_sum(gram[...], width)
    diag[gx, gy] = packed(half + half.T)
    gather_start(*diag_way)
    gather_pass(*diag_way)
    gather_end(*pair_way)
    tiles[:, :, 1:] = pairs[...]
    gather_end(*diag_way)
    tiles[:, :, 0] = diag[...]


def main(basis, reaction):
    ngx, ngy = lax.axis_size("gx"), lax.axis_size("gy")
    width, cx, cy, cz = basis.shape
    yo = LANES // width
    yi = cy // yo
    hbm = pl.BlockSpec(memory_space=pltpu.HBM)
    vmem = pl.BlockSpec(memory_space=pltpu.VMEM)
    field = pltpu.VMEM((cx, yi, cz + 2 * ROWS, LANES), F32)
    tile = (width * width // LANES, LANES)
    one, grid = pltpu.SemaphoreType.DMA((ngy,)), pltpu.SemaphoreType.DMA((ngx, ngy))
    return pl.pallas_call(
        functools.partial(main_kernel, ngx, ngy),
        in_specs=[hbm, hbm],
        out_specs=[vmem, vmem],
        out_shape=[
            jax.ShapeDtypeStruct((cx, yi, LANES, cz), F32),
            jax.ShapeDtypeStruct((ngx, ngy, 4) + tile, F32),
        ],
        scratch_shapes=[
            pltpu.VMEM((cx, cy, cz), F32),
            pltpu.VMEM((3 * cy, yi * LANES), BF16),
            pltpu.VMEM((cx, yi, cz, LANES), F32),
            pltpu.VMEM((4, yi, cz, LANES), F32),
            field, field,
            pltpu.VMEM((4, yi * cz // LANES, 2 * LANES, LANES), BF16),
            pltpu.VMEM((4, 2, yi * cz, LANES), BF16),
            pltpu.VMEM((2 * LANES, 2 * LANES), F32),
            pltpu.VMEM((yi, LANES, cz), F32),
            pltpu.VMEM((cx // yo, LANES, cz), F32),
            pltpu.VMEM((ngx, ngy, 3) + tile, F32),
            pltpu.VMEM((ngx, ngy) + tile, F32),
            pltpu.SemaphoreType.DMA((cx,)),
            pltpu.SemaphoreType.DMA,
            pltpu.SemaphoreType.DMA((3,)),
            pltpu.SemaphoreType.DMA((3,)),
            one, one, grid, grid, one, one, grid, grid,
        ],
        compiler_params=pltpu.CompilerParams(
            collective_id=0, has_side_effects=True, vmem_limit_bytes=40 * 2**20
        ),
        cost_estimate=pl.CostEstimate(
            flops=60 * basis.size, bytes_accessed=8 * basis.size, transcendentals=0
        ),
    )(basis, reaction)


def write_kernel(nat, tiles, extended, coarse, blocks, out_sem, coarse_sem):
    width, cx, cy, cz = extended.shape
    ngx, ngy = tiles.shape[:2]
    yi = nat.shape[1]

    @pl.loop(0, cx)
    def _(x):
        for y in range(cy):
            pltpu.make_async_copy(
                nat.at[x, y % yi, pl.ds((y // yi) * width, width), :],
                extended.at[:, x, y, :],
                out_sem.at[x],
            ).start()

    nothing = jnp.zeros((width, width), F32)

    @pl.loop(0, ngx)
    def _(row):
        for col in range(ngy):
            s = row * ngy + col
            below = jnp.maximum(row - 1, 0)
            blocks[s, 0] = unpacked(tiles[row, col, 0], width)
            lower = unpacked(tiles[below, col, 1], width).T
            blocks[s, 1] = jnp.where(row > 0, lower, 0.0)
            blocks[s, 2] = jnp.where(row < ngx - 1, unpacked(tiles[row, col, 1], width), 0.0)
            blocks[s, 3] = nothing
            if col > 0:
                blocks[s, 3] = unpacked(tiles[row, col - 1, 2] + tiles[row, col, 3], width).T
            blocks[s, 4] = nothing
            if col < ngy - 1:
                blocks[s, 4] = unpacked(tiles[row, col, 2] + tiles[row, col + 1, 3], width)

    copy = pltpu.make_async_copy(blocks, coarse, coarse_sem)
    copy.start()

    @pl.loop(0, cx)
    def _(x):
        pltpu.make_async_copy(nat.at[x], nat.at[x], out_sem.at[x]).wait()

    copy.wait()


def write(nat, tiles, shape):
    width, cx, cy, cz = shape
    ngx, ngy = tiles.shape[:2]
    vmem = pl.BlockSpec(memory_space=pltpu.VMEM)
    hbm = pl.BlockSpec(memory_space=pltpu.HBM)
    coarse = (ngx * ngy, 5, width, width)
    return pl.pallas_call(
        write_kernel,
        in_specs=[vmem, vmem],
        out_specs=[hbm, hbm],
        out_shape=[jax.ShapeDtypeStruct(shape, F32), jax.ShapeDtypeStruct(coarse, F32)],
        scratch_shapes=[
            pltpu.VMEM(coarse, F32),
            pltpu.SemaphoreType.DMA((cx,)),
            pltpu.SemaphoreType.DMA,
        ],
        compiler_params=pltpu.CompilerParams(vmem_limit_bytes=16 * 2**20),
    )(nat, tiles)


def on_device(basis, reaction):
    nat, tiles = main(basis, reaction)
    extended, coarse = write(nat, tiles, basis.shape)
    return extended, coarse


def solution(mesh):
    placed = (P(None, "gx", "gy", None), P("gx", "gy", None))
    return jax.shard_map(
        on_device,
        mesh=mesh,
        in_specs=placed,
        out_specs=(P(None, "gx", "gy", None), P()),
        check_vma=False,
    )
```

time: 55 us -> 43.7 us (0.79)
  Pallas kernels: 49.8 us -> 42 us
  local copies, waits for them, and re-layouts: 4.32 us -> 0.94 us
    pallas_call x1, Pallas kernels: 45.6 us -> 37.3 us  [main(): pl.pallas_call(functools.partial(main_kernel, ngx, ngy), in_specs=[hbm, h...]
    unnamed x4 -> x2, local copies, waits for them, and re-layouts: 4.32 us -> 0.94 us
where the time goes in v2:
time: 43.7 us; the launch traced here: 43.6 us
  Pallas kernels  42 us (96%)
  local copies, waits for them, and re-layouts  0.94 us (2%)
  between operations  0.65 us (1%)
    pallas_call x1, Pallas kernels, main(): pl.pallas_call(functools.partial(main_kernel, ngx, ngy), in_specs=[hbm, h...  37.3 us
    pallas_call x1, Pallas kernels, write(): pl.pallas_call(write_kernel, in_specs=[vmem, vmem], out_specs=[hbm, hbm],...  4.74 us
    unnamed x2, local copies, waits for them, and re-layouts  0.94 us

profile of v2, /device:TPU:0, one launch (start us, length us, event | category | flops | bytes accessed | tf_op | source)
XLA Modules:
  0.0 43.6 jit_solution(15461884379670289405)
XLA Ops:
  0.6 0.0 copy-start
  0.6 0.9 %copy-done = f32[16,16,256]{2,1,0:T(8,128)S(1)} copy-done((f32[16,16,256]{2,1,0:T(8,128)S(1)}, f32[16,16,256]{2,1,0:T(8,128)}, u32[]{:S(2)}) %copy-start) | copy-done | bytes 262168
  1.6 37.3 %shard_map.41 = (f32[16,4,128,256]{3,2,1,0:T(8,128)S(1)}, f32[8,4,4,8,128]{4,3,2,1,0:T(8,128)S(1)}) custom-call(f32[32,16,16,256]{3,2,1,0:T(8,128)} %basis.1, f32[16,16,256]{2,1,0:T(8,128)S(1)} %copy-done), custom_call_target="tpu_custom_call" | custom-call | flops 125829120 | bytes 16777216 | tf_op jit(solution)/shard_map/pallas_call | solution.py:429
  38.8 4.7 %shard_map.42 = (f32[32,16,16,256]{3,2,1,0:T(8,128)}, f32[32,5,32,32]{3,2,1,0:T(8,128)}) custom-call(f32[16,4,128,256]{3,2,1,0:T(8,128)S(1)} %get-tuple-element.4.nat, f32[8,4,4,8,128]{4,3,2,1,0:T(8,128)S(1)} %get-tuple-element.5.tiles), custom_call_target="tpu_custom_call" | custom-call | tf_op jit(solution)/shard_map/pallas_call | solution.py:513
Async XLA Ops:
  0.6 1.0 %copy-start = (f32[16,16,256]{2,1,0:T(8,128)S(1)}, f32[16,16,256]{2,1,0:T(8,128)}, u32[]{:S(2)}) copy-start(f32[16,16,256]{2,1,0:T(8,128)} %reaction.1) | copy-start | bytes 786436

commit v3 on v2

v3 whole, which is shorter than its diff:
```python
import functools

import jax
import jax.numpy as jnp
from jax import lax
from jax.experimental import pallas as pl
from jax.experimental.pallas import tpu as pltpu
from jax.sharding import PartitionSpec as P

SWEEPS = 4
OMEGA = 0.8
ROWS = 8
LANES = 128
MESH = pl.DeviceIdType.MESH
F32 = jnp.float32
BF16 = jnp.bfloat16


def split(value):
    high = value.astype(BF16)
    low = (value - high.astype(F32)).astype(BF16)
    return high, low


def thirds(value):
    first = value.astype(BF16)
    rest = value - first.astype(F32)
    second = rest.astype(BF16)
    third = (rest - second.astype(F32)).astype(BF16)
    return jnp.concatenate([first, second, third], axis=0)


def combined(wide):
    half = wide.shape[0] // 2
    return wide[:half, :half] + wide[:half, half:] + wide[half:, :half]


def block_sum(wide, width):
    full = combined(wide)
    total = full[:width, :width]
    for i in range(width, full.shape[0], width):
        total = total + full[i:i + width, i:i + width]
    return total


def packed(block):
    rows = block.shape[0] * block.shape[1] // LANES
    return jnp.concatenate(
        [block[i:i + rows] for i in range(0, block.shape[0], rows)], axis=1
    )


def unpacked(tile, width):
    return jnp.concatenate(
        [tile[:, i:i + width] for i in range(0, LANES, width)], axis=0
    )


def main_kernel(
    ngx, ngy, basis, reaction, nat, pairs_out, diag_out,
    react, spread, weight, centre, first, second, lefts, rights,
    gram, square, face_x, face_y, pairs, diag,
    in_sem, react_sem, face_send, face_recv, pair_sem, diag_sem,
):
    width, cx, cy, cz = basis.shape
    yo = LANES // width
    yi = cy // yo
    group = cx // yo
    halves = cz // LANES
    ztiles = cz // ROWS
    gx, gy = lax.axis_index("gx"), lax.axis_index("gy")

    lines = nat.reshape(cx, halves, width * cy, LANES)
    count = ngx * ngy
    me = gx * ngy + gy

    def other(d):
        peer = lax.rem(me + d, count)
        return (peer // ngy, lax.rem(peer, ngy))

    barrier = pltpu.get_barrier_semaphore()

    @pl.loop(1, count)
    def _(d):
        pl.semaphore_signal(barrier, inc=1, device_id=other(d), device_id_type=MESH)

    load = pltpu.make_async_copy(reaction, react, react_sem)
    load.start()

    @pl.loop(0, cx)
    def _(x):
        for h in range(halves):
            pltpu.make_async_copy(
                basis.at[:, x, :, h * LANES:(h + 1) * LANES], nat.at[x, h], in_sem.at[x]
            ).start()

    def over_x(peer):
        return pltpu.make_async_remote_copy(
            src_ref=nat.at[0], dst_ref=face_x, send_sem=face_send.at[0], recv_sem=face_recv.at[0],
            device_id=(peer, gy), device_id_type=MESH,
        )

    def over_y(x, upper, peer):
        return pltpu.make_async_remote_copy(
            src_ref=nat.at[x, :, :, cy - 1 if upper else 0, :],
            dst_ref=face_y.at[x // yo, :, pl.ds(lax.rem(x, yo) * width, width), :],
            send_sem=face_send.at[1 + upper], recv_sem=face_recv.at[1 + upper],
            device_id=(gx, peer), device_id_type=MESH,
        )

    middle = (group // 2) * yo

    rows = lax.broadcasted_iota(jnp.int32, (cy, yi * LANES), 0)
    cols = lax.broadcasted_iota(jnp.int32, (cy, yi * LANES), 1)
    chosen = rows == lax.rem(cols, yo) * yi + cols // LANES
    pick = jnp.where(chosen, 1.0, 0.0).astype(BF16)
    spread[...] = jnp.concatenate([pick, pick, pick], axis=0)

    def expanded(values):
        return lax.dot_general(
            thirds(values), spread[...], (((0,), (0,)), ((), ())), preferred_element_type=F32
        )

    line = lax.broadcasted_iota(jnp.int32, (cy, cz), 0)
    face_row = (line == 0) | (line == cy - 1)
    blank = jnp.zeros((ROWS, LANES), F32)
    load.wait()

    def weigh(x):
        wide = expanded(jnp.where(face_row, 0.0, OMEGA / (6.0 + react[x])))
        for j in range(yi):
            weight[x, j] = wide[:, j * LANES:(j + 1) * LANES]

    for x in (1, 2):
        weigh(x)

    @pl.loop(0, cx)
    def _(x):
        for j in range(yi):
            for buffer in (first, second):
                buffer[x, j, 0:ROWS, :] = blank
                buffer[x, j, cz + ROWS:cz + 2 * ROWS, :] = blank

    gram[...] = jnp.zeros_like(gram)

    pl.semaphore_wait(barrier, count - 1)

    lane = lax.broadcasted_iota(jnp.int32, (ROWS, LANES), 1)
    keep = [jnp.full((ROWS, LANES), 1.0 - OMEGA, F32) for _ in range(yi)]
    upper_lane = lax.rem(lane, yo) == yo - 1
    keep[0] = jnp.where(lax.rem(lane, yo) == 0, 1.0, keep[0])
    keep[yi - 1] = jnp.where(upper_lane, 1.0, keep[yi - 1])

    def land(x):
        pltpu.make_async_copy(nat.at[x], nat.at[x], in_sem.at[x]).wait()

        @pl.when((x < middle) & (gy > 0))
        def _():
            over_y(x, 0, gy - 1).start()

        @pl.when((x >= middle) & (gy < ngy - 1))
        def _():
            over_y(x, 1, gy + 1).start()

    def take_in(x, j, h):
        part = lines[x, h, pl.ds(j, LANES, stride=yi), :]
        first[x, j, ROWS + h * LANES:ROWS + (h + 1) * LANES, :] = part.T

    squares = [(j, h) for j in range(yi) for h in range(halves)]

    def line_of(ref, x, t, shift=0):
        return [ref[x, j, pl.ds(ROWS + t * ROWS + shift, ROWS), :] for j in range(yi)]

    def forward(values):
        return pltpu.roll(values[0], LANES - 1, 1)

    def backward(values):
        return pltpu.roll(values[yi - 1], 1, 1)

    def diagonals(here, up):
        inner = [here[j] + up[j + 1] for j in range(yi - 1)]
        return [backward(here) + up[0]] + inner + [here[yi - 1] + forward(up)]

    def finish(source, target, x, t, here, total):
        below, above = line_of(source, x, t, -1), line_of(source, x, t, 1)
        for j in range(yi):
            around = total[j] + (below[j] + above[j])
            target[x, j, pl.ds(ROWS + t * ROWS, ROWS), :] = (
                keep[j] * here[j] + weight[x, j, pl.ds(t * ROWS, ROWS), :] * around
            )

    def sweep_pair(source, target, x, t):
        field = [line_of(source, x + i, t) for i in range(4)]
        for i in range(1, 3):
            down, here, up = field[i - 1:i + 2]
            near = [backward(here)] + here + [forward(here)]
            total = [(down[j] + up[j]) + (near[j] + near[j + 2]) for j in range(yi)]
            finish(source, target, x + i, t, here, total)

    def sweep(source, target):
        @pl.loop(0, ztiles, unroll=2)
        def _(t):
            here = line_of(source, 1, t)
            old = diagonals(line_of(source, 0, t), here)
            for x in range(1, cx - 1):
                up = line_of(source, x + 1, t)
                new = diagonals(here, up)
                total = [old[j + 1] + new[j] for j in range(yi)]
                finish(source, target, x, t, here, total)
                old, here = new, up

    land(0)

    @pl.when(gx > 0)
    def _():
        over_x(gx - 1).start()

    for x in range(4):
        if x:
            land(x)
        for at in squares:
            take_in(x, *at)

    each = ztiles // (2 * len(squares))

    @pl.loop(0, cx - 4, step=2)
    def _(x):
        land(x + 4)
        land(x + 5)
        weigh(x + 3)
        weigh(x + 4)
        for i in range(2):
            for n, at in enumerate(squares):
                take_in(x + 4 + i, *at)
                for m in range(each):
                    sweep_pair(first, second, x, (i * len(squares) + n) * each + m)

    for t in range(ztiles):
        sweep_pair(first, second, cx - 4, t)

    @pl.loop(0, ztiles)
    def _(t):
        for x in (0, cx - 1):
            for j, value in enumerate(line_of(first, x, t)):
                second[x, j, pl.ds(ROWS + t * ROWS, ROWS), :] = value

    sweep(second, first)
    sweep(first, second)

    def joined(ref, start=0, stop=None):
        stop = ref.shape[0] if stop is None else stop
        return jnp.concatenate([ref[i] for i in range(start, stop)], axis=1)

    def couple(start, stop):
        return lax.dot_general(
            joined(lefts.at[0], start, stop), joined(lefts.at[1], start, stop),
            (((1,), (1,)), ((), ())), preferred_element_type=F32,
        )

    def strided_sum(wide):
        square[...] = combined(wide)
        turned = jnp.concatenate(
            [square[pl.ds(g, width, stride=yo), :] for g in range(yo)], axis=0
        ).T
        square[...] = turned
        total = square[pl.ds(0, width, stride=yo), :][:, :width]
        for g in range(1, yo):
            total = total + square[pl.ds(g, width, stride=yo), :][:, g * width:(g + 1) * width]
        return total

    def fill(ref, row, column, value):
        size = value.shape[0]
        for half, part in enumerate(split(value)):
            ref[column, half * LANES + row:half * LANES + row + size] = part

    @pl.when(gx < ngx - 1)
    def _():
        over_x(gx).wait_recv()

    for n, (j, h) in enumerate(squares):
        fill(lefts.at[0], 0, n, face_x.reshape(halves, width * cy, LANES)[h, pl.ds(j, LANES, stride=yi), :])
        fill(lefts.at[1], 0, n, lines[cx - 1, h, pl.ds(j, LANES, stride=yi), :])
    pairs[gx, gy, 0] = packed(-strided_sum(couple(0, len(squares))))

    near, far = face_y.at[pl.ds(0, group // 2)], face_y.at[pl.ds(group // 2, group - group // 2)]

    @pl.when(gy < ngy - 1)
    def _():
        pltpu.make_async_copy(near, near, face_recv.at[1]).wait()

    @pl.when(gy > 0)
    def _():
        pltpu.make_async_copy(far, far, face_recv.at[2]).wait()

    for x in range(cx):
        for h in range(halves):
            own = lines[x, h, pl.ds(cy - 1 if x < middle else 0, width, stride=cy), :]
            at = (x // yo) * halves + h
            fill(lefts.at[0 if x < middle else 1], (x % yo) * width, at, own)
    cut = (group // 2) * halves
    for c in range(group):
        for h in range(halves):
            at = c * halves + h
            fill(lefts.at[1 if at < cut else 0], 0, at, face_y[c, h])
    pairs[gx, gy, 1] = packed(-block_sum(couple(0, cut), width))
    pairs[gx, gy, 2] = packed(-block_sum(couple(cut, group * halves), width))

    @pl.when(gx > 0)
    def _():
        over_x(gx).wait_send()

    @pl.when(gy > 0)
    def _():
        pltpu.make_async_copy(near, near, face_send.at[1]).wait()

    @pl.when(gy < ngy - 1)
    def _():
        pltpu.make_async_copy(far, far, face_send.at[2]).wait()

    def to_y(peer):
        piece = pairs.at[gx, gy]
        return pltpu.make_async_remote_copy(
            src_ref=piece, dst_ref=piece, send_sem=pair_sem.at[0], recv_sem=pair_sem.at[1],
            device_id=(gx, peer), device_id_type=MESH,
        )

    def to_x(peer):
        piece = pairs.at[gx]
        return pltpu.make_async_remote_copy(
            src_ref=piece, dst_ref=piece, send_sem=pair_sem.at[2], recv_sem=pair_sem.at[3],
            device_id=(peer, gy), device_id_type=MESH,
        )

    def to_all(d):
        piece = diag.at[me]
        return pltpu.make_async_remote_copy(
            src_ref=piece, dst_ref=piece, send_sem=diag_sem.at[0], recv_sem=diag_sem.at[1],
            device_id=other(d), device_id_type=MESH,
        )

    def await_bytes(ref, sem):
        pltpu.make_async_copy(ref, ref, sem).wait()

    row_rest, grid_rest = pairs.at[0, pl.ds(0, ngy - 1)], pairs.at[pl.ds(0, ngx - 1)]
    for d in range(1, ngy):
        to_y(lax.rem(gy + d, ngy)).start()

    source, result = second, first

    def applied(x, i, slot, t, last):
        here, above = line_of(result, x, t), line_of(result, x, t, 1)
        up = None if last else line_of(result, x + 1, t)
        edge = jnp.where(upper_lane, 0.0, forward(here))
        beside = here[1:] + [edge]
        out = []
        for j in range(yi):
            total = beside[j] + above[j]
            if up is not None:
                total = total + up[j]
            out.append(centre[slot + i, j, t * ROWS:(t + 1) * ROWS, :] * here[j] - total)
        return out

    def block(x, slot, sweeping=True, last=False):
        for i in range(2):
            wide = expanded(3.0 + 0.5 * react[x + i])
            for j in range(yi):
                centre[slot + i, j] = wide[:, j * LANES:(j + 1) * LANES]
        for n in range(ztiles // 2):
            if sweeping:
                for t in (2 * n, 2 * n + 1):
                    sweep_pair(source, result, x + 2, t)
            for i in range(2):
                two = [applied(x + i, i, slot, t, last and i == 1) for t in (2 * n, 2 * n + 1)]
                for j in range(yi):
                    at = j * cz + n * 2 * ROWS
                    both = jnp.concatenate([two[0][j], two[1][j]], axis=0)
                    for part, value in enumerate(split(both)):
                        rights[slot + i, part, at:at + 2 * ROWS] = value
            i, (j, h) = n // len(squares), squares[n % len(squares)]
            part = result[x + i, j, ROWS + h * LANES:ROWS + (h + 1) * LANES, :].T
            lines[x + i, h, pl.ds(j, LANES, stride=yi), :] = part
            for half, value in enumerate(split(part)):
                lefts[slot + i, j * halves + h, half * LANES:(half + 1) * LANES] = value

    def multiply(slot, fresh=None):
        for i in range(2):
            total = gram[...] + jnp.dot(
                joined(lefts.at[slot + i]), joined(rights.at[slot + i]), preferred_element_type=F32
            )
            gram[...] = total if fresh is None else jnp.where(fresh, 0.0, total)

    for t in range(ztiles):
        sweep_pair(source, result, 0, t)

    steps = (cx - 4) // 4

    @pl.loop(0, steps)
    def _(n):
        @pl.when(n == steps - 1)
        def _():
            await_bytes(row_rest, pair_sem.at[1])
            for d in range(1, ngx):
                to_x(lax.rem(gx + d, ngx)).start()

        multiply(2, n == 0)
        block(4 * n, 0)
        multiply(0)
        block(4 * n + 2, 2)

    multiply(2)
    block(cx - 4, 0, sweeping=False)
    multiply(0)
    block(cx - 2, 2, sweeping=False, last=True)
    multiply(2)

    half = strided_sum(gram[...])
    diag[me] = packed(half + half.T)

    @pl.loop(1, count)
    def _(d):
        to_all(d).start()

    await_bytes(row_rest, pair_sem.at[0])
    await_bytes(grid_rest, pair_sem.at[3])
    await_bytes(grid_rest, pair_sem.at[2])
    pairs_out[...] = pairs[...]
    all_rest = diag.at[pl.ds(0, count - 1)]
    await_bytes(all_rest, diag_sem.at[1])
    await_bytes(all_rest, diag_sem.at[0])
    diag_out[...] = diag[...]


def main(basis, reaction):
    ngx, ngy = lax.axis_size("gx"), lax.axis_size("gy")
    width, cx, cy, cz = basis.shape
    yo = LANES // width
    yi = cy // yo
    hbm = pl.BlockSpec(memory_space=pltpu.HBM)
    vmem = pl.BlockSpec(memory_space=pltpu.VMEM)
    field = pltpu.VMEM((cx, yi, cz + 2 * ROWS, LANES), F32)
    tile = (width * width // LANES, LANES)
    return pl.pallas_call(
        functools.partial(main_kernel, ngx, ngy),
        in_specs=[hbm, hbm],
        out_specs=[vmem, vmem, vmem],
        out_shape=[
            jax.ShapeDtypeStruct((cx, cz // LANES, width, cy, LANES), F32),
            jax.ShapeDtypeStruct((ngx, ngy, 3) + tile, F32),
            jax.ShapeDtypeStruct((ngx * ngy,) + tile, F32),
        ],
        scratch_shapes=[
            pltpu.VMEM((cx, cy, cz), F32),
            pltpu.VMEM((3 * cy, yi * LANES), BF16),
            pltpu.VMEM((cx, yi, cz, LANES), F32),
            pltpu.VMEM((4, yi, cz, LANES), F32),
            field, field,
            pltpu.VMEM((4, yi * cz // LANES, 2 * LANES, LANES), BF16),
            pltpu.VMEM((4, 2, yi * cz, LANES), BF16),
            pltpu.VMEM((2 * LANES, 2 * LANES), F32),
            pltpu.VMEM((LANES, LANES), F32),
            pltpu.VMEM((cz // LANES, width, cy, LANES), F32),
            pltpu.VMEM((cx // yo, cz // LANES, LANES, LANES), F32),
            pltpu.VMEM((ngx, ngy, 3) + tile, F32),
            pltpu.VMEM((ngx * ngy,) + tile, F32),
            pltpu.SemaphoreType.DMA((cx,)),
            pltpu.SemaphoreType.DMA,
            pltpu.SemaphoreType.DMA((3,)),
            pltpu.SemaphoreType.DMA((3,)),
            pltpu.SemaphoreType.DMA((4,)),
            pltpu.SemaphoreType.DMA((2,)),
        ],
        compiler_params=pltpu.CompilerParams(
            collective_id=0, has_side_effects=True, vmem_limit_bytes=40 * 2**20
        ),
        cost_estimate=pl.CostEstimate(
            flops=60 * basis.size, bytes_accessed=8 * basis.size, transcendentals=0
        ),
    )(basis, reaction)


def write_kernel(nat, pairs, diag, extended, coarse, blocks, out_sem, coarse_sem):
    width, cx, cy, cz = extended.shape
    ngx, ngy = pairs.shape[:2]

    @pl.loop(0, cx)
    def _(x):
        for h in range(cz // LANES):
            pltpu.make_async_copy(
                nat.at[x, h], extended.at[:, x, :, h * LANES:(h + 1) * LANES], out_sem
            ).start()

    nothing = jnp.zeros((width, width), F32)

    @pl.loop(0, ngx)
    def _(row):
        for col in range(ngy):
            s = row * ngy + col
            below = jnp.maximum(row - 1, 0)
            blocks[s, 0] = unpacked(diag[s], width)
            lower = unpacked(pairs[below, col, 0], width).T
            blocks[s, 1] = jnp.where(row > 0, lower, 0.0)
            blocks[s, 2] = jnp.where(row < ngx - 1, unpacked(pairs[row, col, 0], width), 0.0)
            blocks[s, 3] = nothing
            if col > 0:
                blocks[s, 3] = unpacked(pairs[row, col - 1, 1] + pairs[row, col, 2], width).T
            blocks[s, 4] = nothing
            if col < ngy - 1:
                blocks[s, 4] = unpacked(pairs[row, col, 1] + pairs[row, col + 1, 2], width)

    copy = pltpu.make_async_copy(blocks, coarse, coarse_sem)
    copy.start()
    pltpu.make_async_copy(nat, nat, out_sem).wait()
    copy.wait()


def write(nat, pairs, diag, shape):
    width = shape[0]
    vmem = pl.BlockSpec(memory_space=pltpu.VMEM)
    hbm = pl.BlockSpec(memory_space=pltpu.HBM)
    coarse = (diag.shape[0], 5, width, width)
    return pl.pallas_call(
        write_kernel,
        in_specs=[vmem, vmem, vmem],
        out_specs=[hbm, hbm],
        out_shape=[jax.ShapeDtypeStruct(shape, F32), jax.ShapeDtypeStruct(coarse, F32)],
        scratch_shapes=[
            pltpu.VMEM(coarse, F32),
            pltpu.SemaphoreType.DMA,
            pltpu.SemaphoreType.DMA,
        ],
        compiler_params=pltpu.CompilerParams(vmem_limit_bytes=16 * 2**20),
    )(nat, pairs, diag)


def on_device(basis, reaction):
    return write(*main(basis, reaction), basis.shape)


def solution(mesh):
    placed = (P(None, "gx", "gy", None), P("gx", "gy", None))
    return jax.shard_map(
        on_device,
        mesh=mesh,
        in_specs=placed,
        out_specs=(P(None, "gx", "gy", None), P()),
        check_vma=False,
    )
```

time: 43.7 us -> 38.1 us (0.87)
  Pallas kernels: 42 us -> 36.3 us
    pallas_call x1, Pallas kernels: 37.3 us -> 32.2 us  [main(): pl.pallas_call(functools.partial(main_kernel, ngx, ngy), in_specs=[hbm, h...]
    pallas_call x1, Pallas kernels: 4.74 us -> 4.14 us  [write(): pl.pallas_call(write_kernel, in_specs=[vmem, vmem, vmem], out_specs=[hbm,...]
where the time goes in v3:
time: 38.1 us; the launch traced here: 37.9 us
  Pallas kernels  36.3 us (95%)
  local copies, waits for them, and re-layouts  0.94 us (2%)
  between operations  0.65 us (2%)
    pallas_call x1, Pallas kernels, main(): pl.pallas_call(functools.partial(main_kernel, ngx, ngy), in_specs=[hbm, h...  32.2 us
    pallas_call x1, Pallas kernels, write(): pl.pallas_call(write_kernel, in_specs=[vmem, vmem, vmem], out_specs=[hbm,...  4.14 us
    unnamed x2, local copies, waits for them, and re-layouts  0.94 us

profile of v3, /device:TPU:0, one launch (start us, length us, event | category | flops | bytes accessed | tf_op | source)
XLA Modules:
  0.0 37.9 jit_solution(5934704067057225944)
XLA Ops:
  0.6 0.0 copy-start
  0.6 0.9 %copy-done = f32[16,16,256]{2,1,0:T(8,128)S(1)} copy-done((f32[16,16,256]{2,1,0:T(8,128)S(1)}, f32[16,16,256]{2,1,0:T(8,128)}, u32[]{:S(2)}) %copy-start) | copy-done | bytes 262168
  1.6 32.2 %shard_map.41 = (f32[16,2,32,16,128]{4,3,2,1,0:T(8,128)S(1)}, f32[8,4,3,8,128]{4,3,2,1,0:T(8,128)S(1)}, f32[32,8,128]{2,1,0:T(8,128)S(1)}) custom-call(f32[32,16,16,256]{3,2,1,0:T(8,128)} %basis.1, f32[16,16,256]{2,1,0:T(8,128)S(1)} %copy-done), custom_call_target="tpu_custom_call" | custom-call | flops 125829120 | bytes 16777216 | tf_op jit(solution)/shard_map/pallas_call | solution.py:442
  33.8 4.1 %shard_map.42 = (f32[32,16,16,256]{3,2,1,0:T(8,128)}, f32[32,5,32,32]{3,2,1,0:T(8,128)}) custom-call(f32[16,2,32,16,128]{4,3,2,1,0:T(8,128)S(1)} %get-tuple-element.5.nat, f32[8,4,3,8,128]{4,3,2,1,0:T(8,128)S(1)} %get-tuple-element.6.pairs, f32[32,8,128]{2,1,0:T(8,128)S(1)} %get-tuple-element.7.diag), custom_call_target="tpu_custom_call" | custom-call | tf_op jit(solution)/shard_map/pallas_call | solution.py:521
Async XLA Ops:
  0.6 1.0 %copy-start = (f32[16,16,256]{2,1,0:T(8,128)S(1)}, f32[16,16,256]{2,1,0:T(8,128)}, u32[]{:S(2)}) copy-start(f32[16,16,256]{2,1,0:T(8,128)} %reaction.1) | copy-start | bytes 786436

commit v4 on v3

--- a/solution.py
+++ b/solution.py
@@ -134,6 +134,11 @@
     for x in (1, 2):
         weigh(x)
 
+    @pl.loop(0, ztiles + 2)
+    def _(t):
+        for j in range(yi):
+            first[cx, j, pl.ds(t * ROWS, ROWS), :] = blank
+
     @pl.loop(0, cx)
     def _(x):
         for j in range(yi):
@@ -143,8 +148,6 @@
 
     gram[...] = jnp.zeros_like(gram)
 
-    pl.semaphore_wait(barrier, count - 1)
-
     lane = lax.broadcasted_iota(jnp.int32, (ROWS, LANES), 1)
     keep = [jnp.full((ROWS, LANES), 1.0 - OMEGA, F32) for _ in range(yi)]
     upper_lane = lax.rem(lane, yo) == yo - 1
@@ -153,14 +156,6 @@
 
     def land(x):
         pltpu.make_async_copy(nat.at[x], nat.at[x], in_sem.at[x]).wait()
-
-        @pl.when((x < middle) & (gy > 0))
-        def _():
-            over_y(x, 0, gy - 1).start()
-
-        @pl.when((x >= middle) & (gy < ngy - 1))
-        def _():
-            over_y(x, 1, gy + 1).start()
 
     def take_in(x, j, h):
         part = lines[x, h, pl.ds(j, LANES, stride=yi), :]
@@ -209,15 +204,8 @@
                 finish(source, target, x, t, here, total)
                 old, here = new, up
 
-    land(0)
-
-    @pl.when(gx > 0)
-    def _():
-        over_x(gx - 1).start()
-
     for x in range(4):
-        if x:
-            land(x)
+        land(x)
         for at in squares:
             take_in(x, *at)
 
@@ -235,6 +223,24 @@
                 for m in range(each):
                     sweep_pair(first, second, x, (i * len(squares) + n) * each + m)
 
+    pl.semaphore_wait(barrier, count - 1)
+
+    @pl.when(gx > 0)
+    def _():
+        over_x(gx - 1).start()
+
+    @pl.when(gy > 0)
+    def _():
+        @pl.loop(0, middle)
+        def _(x):
+            over_y(x, 0, gy - 1).start()
+
+    @pl.when(gy < ngy - 1)
+    def _():
+        @pl.loop(middle, cx)
+        def _(x):
+            over_y(x, 1, gy + 1).start()
+
     for t in range(ztiles):
         sweep_pair(first, second, cx - 4, t)
 
@@ -246,6 +252,7 @@
 
     sweep(second, first)
     sweep(first, second)
+    sweep(second, first)
 
     def joined(ref, start=0, stop=None):
         stop = ref.shape[0] if stop is None else stop
@@ -345,32 +352,26 @@
     for d in range(1, ngy):
         to_y(lax.rem(gy + d, ngy)).start()
 
-    source, result = second, first
-
-    def applied(x, i, slot, t, last):
+    result = first
+
+    def applied(x, slot, t):
         here, above = line_of(result, x, t), line_of(result, x, t, 1)
-        up = None if last else line_of(result, x + 1, t)
+        up = line_of(result, x + 1, t)
         edge = jnp.where(upper_lane, 0.0, forward(here))
         beside = here[1:] + [edge]
-        out = []
-        for j in range(yi):
-            total = beside[j] + above[j]
-            if up is not None:
-                total = total + up[j]
-            out.append(centre[slot + i, j, t * ROWS:(t + 1) * ROWS, :] * here[j] - total)
-        return out
-
-    def block(x, slot, sweeping=True, last=False):
+        return [
+            centre[slot, j, t * ROWS:(t + 1) * ROWS, :] * here[j] - (beside[j] + above[j] + up[j])
+            for j in range(yi)
+        ]
+
+    def block(x, slot):
         for i in range(2):
             wide = expanded(3.0 + 0.5 * react[x + i])
             for j in range(yi):
                 centre[slot + i, j] = wide[:, j * LANES:(j + 1) * LANES]
         for n in range(ztiles // 2):
-            if sweeping:
-                for t in (2 * n, 2 * n + 1):
-                    sweep_pair(source, result, x + 2, t)
             for i in range(2):
-                two = [applied(x + i, i, slot, t, last and i == 1) for t in (2 * n, 2 * n + 1)]
+                two = [applied(x + i, slot + i, t) for t in (2 * n, 2 * n + 1)]
                 for j in range(yi):
                     at = j * cz + n * 2 * ROWS
                     both = jnp.concatenate([two[0][j], two[1][j]], axis=0)
@@ -389,14 +390,11 @@
             )
             gram[...] = total if fresh is None else jnp.where(fresh, 0.0, total)
 
-    for t in range(ztiles):
-        sweep_pair(source, result, 0, t)
-
-    steps = (cx - 4) // 4
+    steps = cx // 4
 
     @pl.loop(0, steps)
     def _(n):
-        @pl.when(n == steps - 1)
+        @pl.when(n == steps // 2)
         def _():
             await_bytes(row_rest, pair_sem.at[1])
             for d in range(1, ngx):
@@ -407,10 +405,6 @@
         multiply(0)
         block(4 * n + 2, 2)
 
-    multiply(2)
-    block(cx - 4, 0, sweeping=False)
-    multiply(0)
-    block(cx - 2, 2, sweeping=False, last=True)
     multiply(2)
 
     half = strided_sum(gram[...])
@@ -437,7 +431,7 @@
     yi = cy // yo
     hbm = pl.BlockSpec(memory_space=pltpu.HBM)
     vmem = pl.BlockSpec(memory_space=pltpu.VMEM)
-    field = pltpu.VMEM((cx, yi, cz + 2 * ROWS, LANES), F32)
+    field = [pltpu.VMEM((cx + i, yi, cz + 2 * ROWS, LANES), F32) for i in (1, 0)]
     tile = (width * width // LANES, LANES)
     return pl.pallas_call(
         functools.partial(main_kernel, ngx, ngy),
@@ -453,7 +447,7 @@
             pltpu.VMEM((3 * cy, yi * LANES), BF16),
             pltpu.VMEM((cx, yi, cz, LANES), F32),
             pltpu.VMEM((4, yi, cz, LANES), F32),
-            field, field,
+            *field,
             pltpu.VMEM((4, yi * cz // LANES, 2 * LANES, LANES), BF16),
             pltpu.VMEM((4, 2, yi * cz, LANES), BF16),
             pltpu.VMEM((2 * LANES, 2 * LANES), F32),

time: 38.1 us -> 36.8 us (0.966)
  Pallas kernels: 36.3 us -> 35.1 us
    pallas_call x1, Pallas kernels: 32.2 us -> 30.9 us  [main(): pl.pallas_call(functools.partial(main_kernel, ngx, ngy), in_specs=[hbm, h...]
where the time goes in v4:
time: 36.8 us; the launch traced here: 36.7 us
  Pallas kernels  35.1 us (95%)
  local copies, waits for them, and re-layouts  0.94 us (3%)
  between operations  0.65 us (2%)
    pallas_call x1, Pallas kernels, main(): pl.pallas_call(functools.partial(main_kernel, ngx, ngy), in_specs=[hbm, h...  30.9 us
    pallas_call x1, Pallas kernels, write(): pl.pallas_call(write_kernel, in_specs=[vmem, vmem, vmem], out_specs=[hbm,...  4.14 us
    unnamed x2, local copies, waits for them, and re-layouts  0.94 us

profile of v4, /device:TPU:0, one launch (start us, length us, event | category | flops | bytes accessed | tf_op | source)
XLA Modules:
  0.0 36.7 jit_solution(455385650264491181)
XLA Ops:
  0.6 0.0 copy-start
  0.6 0.9 %copy-done = f32[16,16,256]{2,1,0:T(8,128)S(1)} copy-done((f32[16,16,256]{2,1,0:T(8,128)S(1)}, f32[16,16,256]{2,1,0:T(8,128)}, u32[]{:S(2)}) %copy-start) | copy-done | bytes 262168
  1.6 30.9 %shard_map.41 = (f32[16,2,32,16,128]{4,3,2,1,0:T(8,128)S(1)}, f32[8,4,3,8,128]{4,3,2,1,0:T(8,128)S(1)}, f32[32,8,128]{2,1,0:T(8,128)S(1)}) custom-call(f32[32,16,16,256]{3,2,1,0:T(8,128)} %basis.1, f32[16,16,256]{2,1,0:T(8,128)S(1)} %copy-done), custom_call_target="tpu_custom_call" | custom-call | flops 125829120 | bytes 16777216 | tf_op jit(solution)/shard_map/pallas_call | solution.py:436
  32.5 4.1 %shard_map.42 = (f32[32,16,16,256]{3,2,1,0:T(8,128)}, f32[32,5,32,32]{3,2,1,0:T(8,128)}) custom-call(f32[16,2,32,16,128]{4,3,2,1,0:T(8,128)S(1)} %get-tuple-element.5.nat, f32[8,4,3,8,128]{4,3,2,1,0:T(8,128)S(1)} %get-tuple-element.6.pairs, f32[32,8,128]{2,1,0:T(8,128)S(1)} %get-tuple-element.7.diag), custom_call_target="tpu_custom_call" | custom-call | tf_op jit(solution)/shard_map/pallas_call | solution.py:515
Async XLA Ops:
  0.6 1.0 %copy-start = (f32[16,16,256]{2,1,0:T(8,128)S(1)}, f32[16,16,256]{2,1,0:T(8,128)}, u32[]{:S(2)}) copy-start(f32[16,16,256]{2,1,0:T(8,128)} %reaction.1) | copy-start | bytes 786436

commit v5 on v4

--- a/solution.py
+++ b/solution.py
@@ -74,15 +74,9 @@
     count = ngx * ngy
     me = gx * ngy + gy
 
-    def other(d):
-        peer = lax.rem(me + d, count)
-        return (peer // ngy, lax.rem(peer, ngy))
-
-    barrier = pltpu.get_barrier_semaphore()
-
-    @pl.loop(1, count)
-    def _(d):
-        pl.semaphore_signal(barrier, inc=1, device_id=other(d), device_id_type=MESH)
+    columns = [lax.rem(gx + d, ngx) for d in range(1, ngx)] + [gx]
+    planes = [lax.rem(gy + d, ngy) for d in range(1, ngy)] + [gy]
+    others = [(column, plane) for column in columns for plane in planes][:-1]
 
     load = pltpu.make_async_copy(reaction, react, react_sem)
     load.start()
@@ -94,6 +88,10 @@
                 basis.at[:, x, :, h * LANES:(h + 1) * LANES], nat.at[x, h], in_sem.at[x]
             ).start()
 
+    barrier = pltpu.get_barrier_semaphore()
+    for peer in others:
+        pl.semaphore_signal(barrier, inc=1, device_id=peer, device_id_type=MESH)
+
     def over_x(peer):
         return pltpu.make_async_remote_copy(
             src_ref=nat.at[0], dst_ref=face_x, send_sem=face_send.at[0], recv_sem=face_recv.at[0],
@@ -124,15 +122,10 @@
     line = lax.broadcasted_iota(jnp.int32, (cy, cz), 0)
     face_row = (line == 0) | (line == cy - 1)
     blank = jnp.zeros((ROWS, LANES), F32)
-    load.wait()
-
     def weigh(x):
         wide = expanded(jnp.where(face_row, 0.0, OMEGA / (6.0 + react[x])))
         for j in range(yi):
             weight[x, j] = wide[:, j * LANES:(j + 1) * LANES]
-
-    for x in (1, 2):
-        weigh(x)
 
     @pl.loop(0, ztiles + 2)
     def _(t):
@@ -209,6 +202,9 @@
         for at in squares:
             take_in(x, *at)
 
+    load.wait()
+    for x in (1, 2):
+        weigh(x)
     each = ztiles // (2 * len(squares))
 
     @pl.loop(0, cx - 4, step=2)
@@ -258,9 +254,9 @@
         stop = ref.shape[0] if stop is None else stop
         return jnp.concatenate([ref[i] for i in range(start, stop)], axis=1)
 
-    def couple(start, stop):
+    def couple(slot, start, stop):
         return lax.dot_general(
-            joined(lefts.at[0], start, stop), joined(lefts.at[1], start, stop),
+            joined(lefts.at[slot], start, stop), joined(lefts.at[slot + 1], start, stop),
             (((1,), (1,)), ((), ())), preferred_element_type=F32,
         )
 
@@ -284,33 +280,33 @@
     def _():
         over_x(gx).wait_recv()
 
+    near, far = face_y.at[pl.ds(0, group // 2)], face_y.at[pl.ds(group // 2, group - group // 2)]
+
+    @pl.when(gy < ngy - 1)
+    def _():
+        pltpu.make_async_copy(near, near, face_recv.at[1]).wait()
+
+    @pl.when(gy > 0)
+    def _():
+        pltpu.make_async_copy(far, far, face_recv.at[2]).wait()
+
     for n, (j, h) in enumerate(squares):
         fill(lefts.at[0], 0, n, face_x.reshape(halves, width * cy, LANES)[h, pl.ds(j, LANES, stride=yi), :])
         fill(lefts.at[1], 0, n, lines[cx - 1, h, pl.ds(j, LANES, stride=yi), :])
-    pairs[gx, gy, 0] = packed(-strided_sum(couple(0, len(squares))))
-
-    near, far = face_y.at[pl.ds(0, group // 2)], face_y.at[pl.ds(group // 2, group - group // 2)]
-
-    @pl.when(gy < ngy - 1)
-    def _():
-        pltpu.make_async_copy(near, near, face_recv.at[1]).wait()
-
-    @pl.when(gy > 0)
-    def _():
-        pltpu.make_async_copy(far, far, face_recv.at[2]).wait()
+    pairs[gx, gy, 0] = packed(-strided_sum(couple(0, 0, len(squares))))
 
     for x in range(cx):
         for h in range(halves):
             own = lines[x, h, pl.ds(cy - 1 if x < middle else 0, width, stride=cy), :]
             at = (x // yo) * halves + h
-            fill(lefts.at[0 if x < middle else 1], (x % yo) * width, at, own)
+            fill(lefts.at[2 if x < middle else 3], (x % yo) * width, at, own)
     cut = (group // 2) * halves
     for c in range(group):
         for h in range(halves):
             at = c * halves + h
-            fill(lefts.at[1 if at < cut else 0], 0, at, face_y[c, h])
-    pairs[gx, gy, 1] = packed(-block_sum(couple(0, cut), width))
-    pairs[gx, gy, 2] = packed(-block_sum(couple(cut, group * halves), width))
+            fill(lefts.at[3 if at < cut else 2], 0, at, face_y[c, h])
+    pairs[gx, gy, 1] = packed(-block_sum(couple(2, 0, cut), width))
+    pairs[gx, gy, 2] = packed(-block_sum(couple(2, cut, group * halves), width))
 
     @pl.when(gx > 0)
     def _():
@@ -338,19 +334,19 @@
             device_id=(peer, gy), device_id_type=MESH,
         )
 
-    def to_all(d):
+    def to_other(peer):
         piece = diag.at[me]
         return pltpu.make_async_remote_copy(
             src_ref=piece, dst_ref=piece, send_sem=diag_sem.at[0], recv_sem=diag_sem.at[1],
-            device_id=other(d), device_id_type=MESH,
+            device_id=peer, device_id_type=MESH,
         )
 
     def await_bytes(ref, sem):
         pltpu.make_async_copy(ref, ref, sem).wait()
 
     row_rest, grid_rest = pairs.at[0, pl.ds(0, ngy - 1)], pairs.at[pl.ds(0, ngx - 1)]
-    for d in range(1, ngy):
-        to_y(lax.rem(gy + d, ngy)).start()
+    for plane in planes[:-1]:
+        to_y(plane).start()
 
     result = first
 
@@ -397,8 +393,8 @@
         @pl.when(n == steps // 2)
         def _():
             await_bytes(row_rest, pair_sem.at[1])
-            for d in range(1, ngx):
-                to_x(lax.rem(gx + d, ngx)).start()
+            for column in columns[:-1]:
+                to_x(column).start()
 
         multiply(2, n == 0)
         block(4 * n, 0)
@@ -410,9 +406,8 @@
     half = strided_sum(gram[...])
     diag[me] = packed(half + half.T)
 
-    @pl.loop(1, count)
-    def _(d):
-        to_all(d).start()
+    for peer in others:
+        to_other(peer).start()
 
     await_bytes(row_rest, pair_sem.at[0])
     await_bytes(grid_rest, pair_sem.at[3])
@@ -469,7 +464,7 @@
         cost_estimate=pl.CostEstimate(
             flops=60 * basis.size, bytes_accessed=8 * basis.size, transcendentals=0
         ),
-    )(basis, reaction)
+    )(basis, pltpu.with_memory_space_constraint(reaction, pltpu.HBM))
 
 
 def write_kernel(nat, pairs, diag, extended, coarse, blocks, out_sem, coarse_sem):

time: 36.8 us -> 35.7 us (0.970)
  local copies, waits for them, and re-layouts: 0.94 us -> 0 us
    unnamed x2 -> x0, local copies, waits for them, and re-layouts: 0.94 us -> none
where the time goes in v5:
time: 35.7 us; the launch traced here: 35.5 us
  Pallas kernels  34.9 us (98%)
  between operations  0.64 us (2%)
    pallas_call x1, Pallas kernels, main(): pl.pallas_call(functools.partial(main_kernel, ngx, ngy), in_specs=[hbm, h...  30.8 us
    pallas_call x1, Pallas kernels, write(): pl.pallas_call(write_kernel, in_specs=[vmem, vmem, vmem], out_specs=[hbm,...  4.14 us

profile of v5, /device:TPU:0, one launch (start us, length us, event | category | flops | bytes accessed | tf_op | source)
XLA Modules:
  0.0 35.5 jit_solution(15924781252927500431)
XLA Ops:
  0.6 30.8 %shard_map.41 = (f32[16,2,32,16,128]{4,3,2,1,0:T(8,128)S(1)}, f32[8,4,3,8,128]{4,3,2,1,0:T(8,128)S(1)}, f32[32,8,128]{2,1,0:T(8,128)S(1)}) custom-call(f32[32,16,16,256]{3,2,1,0:T(8,128)} %basis.1, f32[16,16,256]{2,1,0:T(8,128)} %reaction.1), custom_call_target="tpu_custom_call" | custom-call | flops 125829120 | bytes 16777216 | tf_op jit(solution)/shard_map/pallas_call | solution.py:431
  31.4 4.1 %shard_map.42 = (f32[32,16,16,256]{3,2,1,0:T(8,128)}, f32[32,5,32,32]{3,2,1,0:T(8,128)}) custom-call(f32[16,2,32,16,128]{4,3,2,1,0:T(8,128)S(1)} %get-tuple-element.5.nat, f32[8,4,3,8,128]{4,3,2,1,0:T(8,128)S(1)} %get-tuple-element.6.pairs, f32[32,8,128]{2,1,0:T(8,128)S(1)} %get-tuple-element.7.diag), custom_call_target="tpu_custom_call" | custom-call | tf_op jit(solution)/shard_map/pallas_call | solution.py:510
